TPU v7x, 128 devices: a whole 4x4x4 slice. The times are simulated.
128 devices in a mesh: slab: 32 (over z, y, core), plane: 4 (over x).
Axes of the slice: x: 4, y: 4, z: 4, core: 2. Of those that a mesh axis runs over, the one named last changes fastest.
Arguments:
- tissue_v: float32 [128, 64, 128], P('slab', 'plane'), may hold values from -4 to 4
- tissue_gates: float32 [40, 128, 64, 128], P(None, 'slab', 'plane'), may hold values from 0 to 1
- tissue_diff: float32 [128, 64, 128], P('slab', 'plane'), may hold values from 0.2 to 1
- fibre_v: float32 [512, 2048], P('slab', 'plane'), may hold values from -4 to 4
- fibre_gates: float32 [40, 512, 2048], P(None, 'slab', 'plane'), may hold values from 0 to 1
- fibre_diff: float32 [512, 2048], P('slab', 'plane'), may hold values from 0.2 to 1
- gate_half: float32 [40], replicated, may hold values from -3 to 3
- gate_rate: float32 [40], replicated, may hold values from 0.5 to 20
- gate_cond: float32 [40], replicated, may hold values from 0.01 to 0.15
- gate_rev: float32 [40], replicated, may hold values from -2 to 2
- junc_cond: float32 [8], replicated, may hold values from 0.25 to 2
- junc_fibre: int32 [524288], P(('slab', 'plane')), may hold values from 0 to 15
- junc_fcell: int32 [524288], P(('slab', 'plane')), may hold values from 0 to 511
- junc_owner: int32 [524288, 1], P(('slab', 'plane')), may hold values from 0 to 127; in each aligned block of 4096 rows (0 to 4095, 4096 to 8191, ...) at most 64 rows name the same one
- junc_tcell: int32 [524288], P(('slab', 'plane')), may hold values from 0 to 8191
- junc_class: int32 [524288], P(('slab', 'plane')), may hold values from 0 to 7
Outputs:
- tissue_out: float32 [128, 64, 128], P('slab', 'plane')
- fibre_out: float32 [512, 2048], P('slab', 'plane')
Inputs may be any that keep to these rules, and one draw needn't show every extreme that they name: `junc_owner`: among the junctions held by one device, no tissue block is named by more than 64 of them, and some block is named by exactly 64. `junc_fibre`: A fibre of the slab group of the device that holds the junction. `junc_fcell`: A cell of the holding device's share of that fibre. `junc_tcell`: numbered over the owner's block in the order z, y, x with x fastest.
All inputs are finite; a program needn't handle non-finite values.
Results may differ from a plain program's by a relative error of at most 0.00005.
Values sent between devices are 32-bit elements; how exact they have to be, the bound alone decides.
A program may use at most 64 MiB of HBM per device.

v0:
```python
import jax
import jax.numpy as jnp
from jax import lax
from jax.sharding import PartitionSpec as P

STEPS = 14


time_step = 0.1
gate_slope = 2.0


def extended(array, sides, width):
    edges = {}
    for axis, dim in sides:
        peers, length = (lax.axis_size(axis), array.shape[dim])
        up = [(i, (i + 1) % peers) for i in range(peers - 1)]
        last = lax.slice_in_dim(array, length - width, length, axis=dim)
        first = lax.slice_in_dim(array, 0, width, axis=dim)
        edges[dim] = (
            lax.ppermute(last, axis, up),
            lax.ppermute(first, axis, [(b, a) for a, b in up]),
        )
    done = []
    for _, dim in sides:
        low, high = edges[dim]
        around = [(width, width) if d in done else (0, 0) for d in range(array.ndim)]
        array = jnp.concatenate([jnp.pad(low, around), array, jnp.pad(high, around)], axis=dim)
        done.append(dim)
    return array


def with_halo(block, sides, width):
    for axis, dim in sides:
        count = lax.axis_size(axis)
        forward = [(i, i + 1) for i in range(count - 1)]
        backward = [(target, source) for source, target in forward]
        low = lax.ppermute(
            lax.slice_in_dim(block, block.shape[dim] - width, None, axis=dim), axis, forward
        )
        high = lax.ppermute(lax.slice_in_dim(block, 0, width, axis=dim), axis, backward)
        block = jnp.concatenate([low, block, high], axis=dim)
    return block


def membrane(voltage, gates, gate_half, gate_rate, gate_cond, gate_rev):
    gate_shape = (gates.shape[0],) + (1,) * (gates.ndim - 1)
    gate_signs = (
        jnp.where(jnp.arange(gates.shape[0], dtype=jnp.int32) % 2 == 0, 1.0, -1.0)
        .astype(jnp.float32)
        .reshape(gate_shape)
    )
    shifted = voltage[None] - gate_half.reshape(gate_shape)
    steady = jax.nn.sigmoid(gate_signs * gate_slope * shifted)
    decay_factor = jnp.exp(
        -time_step * gate_rate.reshape(gate_shape) * (1.0 + jax.nn.sigmoid(shifted))
    )
    renewed = steady + (gates - steady) * decay_factor
    conduct = jnp.tensordot(gate_cond, renewed, axes=1, precision=lax.Precision.HIGHEST)
    driven = jnp.tensordot(gate_cond * gate_rev, renewed, axes=1, precision=lax.Precision.HIGHEST)
    return (renewed, voltage * conduct - driven)


def line_count(length, offset, total):
    places = offset + jnp.arange(length, dtype=jnp.int32)
    return (places > 0).astype(jnp.float32) + (places < total - 1).astype(jnp.float32)


def class_gain(classes, junc_cond):
    return jnp.sum(
        jnp.where(
            classes[:, None] == jnp.arange(junc_cond.shape[0], dtype=jnp.int32)[None, :],
            junc_cond[None, :],
            jnp.zeros((), jnp.float32),
        ),
        axis=1,
    )


def make_onehot(indices, count):
    return (indices[:, None] == jnp.arange(count, dtype=jnp.int32)[None, :]).astype(jnp.float32)


def pick_values(row_onehot, col_onehot, table):
    rows_read = jnp.dot(
        row_onehot, table, precision=lax.Precision.HIGHEST, preferred_element_type=jnp.float32
    )
    return jnp.sum(rows_read * col_onehot, axis=1)


def place_values(row_onehot, col_onehot, values):
    weighted = col_onehot * values[:, None]
    return lax.dot_general(
        row_onehot,
        weighted,
        (((0,), (0,)), ((), ())),
        precision=lax.Precision.HIGHEST,
        preferred_element_type=jnp.float32,
    )


def trade_both(paired):
    return lax.all_to_all(paired, ("slab", "plane"), split_axis=1, concat_axis=1, tiled=True)


def body(
    tissue_v,
    tissue_gates,
    tissue_diff,
    fibre_v,
    fibre_gates,
    fibre_diff,
    gate_half,
    gate_rate,
    gate_cond,
    gate_rev,
    junc_cond,
    junc_fibre,
    junc_fcell,
    junc_owner,
    junc_tcell,
    junc_class,
):
    slab_count = lax.axis_size("slab")
    plane_count = lax.axis_size("plane")
    devices = slab_count * plane_count
    layers_dev, rows_dev, cols_dev = tissue_v.shape
    fibre_rows, fibre_cols = fibre_v.shape
    junctions = junc_fibre.shape[0]
    capacity = 2 * junctions // devices
    tissue_count = (
        line_count(layers_dev, lax.axis_index("slab") * layers_dev, layers_dev * slab_count)[
            :, None, None
        ]
        + line_count(rows_dev, lax.axis_index("plane") * rows_dev, rows_dev * plane_count)[
            None, :, None
        ]
        + line_count(cols_dev, 0, cols_dev)[None, None, :]
    )
    fibre_count = line_count(
        fibre_cols, lax.axis_index("plane") * fibre_cols, fibre_cols * plane_count
    )[None, :]
    fibre_cells = fibre_rows * fibre_cols
    fibre_width = 128
    fibre_grid_rows = fibre_cells // fibre_width
    tissue_grid_rows = layers_dev * rows_dev
    owners = junc_owner[:, 0]
    owner_onehot = make_onehot(owners, devices)
    owner_table = owner_onehot.astype(jnp.int32)
    slot_rank = jnp.sum(jnp.cumsum(owner_table, axis=0) * owner_table, axis=1) - 1
    rank_onehot = make_onehot(slot_rank, capacity)
    slot_index = owners * capacity + slot_rank
    fibre_index = junc_fibre * fibre_cols + junc_fcell
    fibre_row_onehot = make_onehot(fibre_index // fibre_width, fibre_grid_rows)
    fibre_col_onehot = make_onehot(fibre_index % fibre_width, fibre_width)
    cell_table = jnp.zeros((devices * capacity,), jnp.int32).at[slot_index].set(junc_tcell)
    class_table = jnp.full((devices * capacity,), -1, jnp.int32).at[slot_index].set(junc_class)
    sent_tables = jnp.stack([cell_table, class_table]).reshape(2, devices, capacity)
    got_tables = lax.all_to_all(
        sent_tables, ("slab", "plane"), split_axis=1, concat_axis=1, tiled=True
    )
    remote_cells = got_tables[0].reshape(-1)
    remote_gain = class_gain(got_tables[1].reshape(-1), junc_cond)
    own_gain = class_gain(junc_class, junc_cond)
    cell_row_onehot = make_onehot(remote_cells // cols_dev, tissue_grid_rows)
    cell_col_onehot = make_onehot(remote_cells % cols_dev, cols_dev)

    def advance(step_index, carry):
        tissue_now, tissue_state, fibre_now, fibre_state = carry
        fibre_grid = fibre_now.reshape(fibre_grid_rows, fibre_width)
        tissue_grid = tissue_now.reshape(tissue_grid_rows, cols_dev)
        fibre_at_junction = pick_values(fibre_row_onehot, fibre_col_onehot, fibre_grid)
        outgoing = place_values(owner_onehot, rank_onehot, fibre_at_junction)
        tissue_at_slot = pick_values(cell_row_onehot, cell_col_onehot, tissue_grid)
        paired = jnp.stack([outgoing, tissue_at_slot.reshape(devices, capacity)])
        traded = trade_both(paired)
        current = remote_gain * (traded[0].reshape(-1) - tissue_at_slot)
        fibre_current = own_gain * (
            fibre_at_junction - pick_values(owner_onehot, rank_onehot, traded[1])
        )
        tissue_source = place_values(cell_row_onehot, cell_col_onehot, current).reshape(
            tissue_now.shape
        )
        fibre_source = place_values(fibre_row_onehot, fibre_col_onehot, fibre_current).reshape(
            fibre_now.shape
        )
        padded = extended(tissue_now, (("slab", 0), ("plane", 1)), 1)
        sides = jnp.pad(tissue_now, ((0, 0), (0, 0), (1, 1)))
        neighbours = (
            padded[2:, 1:-1]
            + padded[:-2, 1:-1]
            + padded[1:-1, 2:]
            + padded[1:-1, :-2]
            + sides[:, :, 2:]
            + sides[:, :, :-2]
        )
        tissue_lap = neighbours - tissue_count * tissue_now
        fibre_padded = with_halo(fibre_now, (("plane", 1),), 1)
        fibre_lap = fibre_padded[:, 2:] + fibre_padded[:, :-2] - fibre_count * fibre_now
        tissue_state, tissue_ionic = membrane(
            tissue_now, tissue_state, gate_half, gate_rate, gate_cond, gate_rev
        )
        fibre_state, fibre_ionic = membrane(
            fibre_now, fibre_state, gate_half, gate_rate, gate_cond, gate_rev
        )
        tissue_next = tissue_now + time_step * (
            tissue_diff * tissue_lap - tissue_ionic + tissue_source
        )
        fibre_next = fibre_now + time_step * (fibre_diff * fibre_lap - fibre_ionic - fibre_source)
        return (tissue_next, tissue_state, fibre_next, fibre_state)

    final = lax.fori_loop(0, STEPS, advance, (tissue_v, tissue_gates, fibre_v, fibre_gates))
    return (final[0], final[2])


def solution(mesh):
    in_specs = (
        P("slab", "plane", None),
        P(None, "slab", "plane", None),
        P("slab", "plane", None),
        P("slab", "plane"),
        P(None, "slab", "plane"),
        P("slab", "plane"),
        P(),
        P(),
        P(),
        P(),
        P(),
        P(("slab", "plane")),
        P(("slab", "plane")),
        P(("slab", "plane"), None),
        P(("slab", "plane")),
        P(("slab", "plane")),
    )
    out_specs = (P("slab", "plane", None), P("slab", "plane"))
    return jax.shard_map(body, mesh=mesh, in_specs=in_specs, out_specs=out_specs, check_vma=False)
```

profile of v0, /device:TPU:1, one launch (start us, length us, event | category | flops | bytes accessed | tf_op | source)
XLA Modules:
  0.0 869.6 jit_solution(15111886859840716385)
XLA Ops:
  5.3 15.9 %scatter_custom_fusion = s32[8192]{0:T(1024)S(1)} fusion(s32[4096]{0:T(1024)S(1)} %bitcast.121, s32[4096]{0:T(1024)} %param.32, s32[]{:T(128)} %copy.102), kind=kCustom, calls=%fused_computation.175 | custom fusion | bytes 33280 | tf_op jit(solution)/shard_map/scatter | solution.py:156
  21.2 15.5 %scatter_custom_fusion.1 = s32[8192]{0:T(1024)S(1)} fusion(s32[4096]{0:T(1024)S(1)} %bitcast.122, s32[4096]{0:T(1024)S(1)} %copy-done.11, s32[]{:T(128)} %constant.147.clone.1), kind=kCustom, calls=%fused_computation.173 | custom fusion | bytes 32772 | tf_op jit(solution)/shard_map/scatter | solution.py:157
  38.0 11.5 %all-to-all-start.1 = ((s32[128,1,128]{2,1,0:T(1,128)}), s32[128,1,128]{2,1,0:T(1,128)S(1)}, u32[]{:S(2)}, u32[]{:S(2)}) async-start(s32[128,1,128]{2,1,0:T(1,128)} %reshape.328), calls=%async_computation.1 | async-start | bytes 131072 | tf_op jit(solution)/shard_map/all_to_all | solution.py:159
  49.5 9.7 %all-to-all-done.1 = s32[128,1,128]{2,1,0:T(1,128)S(1)} async-done(((s32[128,1,128]{2,1,0:T(1,128)}), s32[128,1,128]{2,1,0:T(1,128)S(1)}, u32[]{:S(2)}, u32[]{:S(2)}) %all-to-all-start.1) | async-done | bytes 65568 | tf_op jit(solution)/shard_map/all_to_all | solution.py:159
  61.4 807.5 %while.19 = (s32[]{:T(128)}, f32[4,16,128]{2,1,0:T(8,128)S(1)}, f32[40,4,16,128]{3,2,1,0:T(8,128)S(1)}, f32[16,512]{1,0:T(8,128)S(1)}, f32[40,16,512]{2,1,0:T(8,...) while((s32[]{:T(128)}, f32[4,16,128]{2,1,0:T(8,128)S(1)}, ...), condition=%wide.region_11.12_spmd.clone, body=%wide.region_7.11_spmd.clone.sunk | while | flops 3260222976 | bytes 13602965 | solution.py:212
  61.7 4.1 fusion.203
  71.2 4.2 all-to-all-start
  85.5 4.0 collective-permute-start.4
  107.5 4.6 fusion.207
  112.3 4.1 fusion.203
  121.8 11.9 %all-to-all-start = ((f32[128,1,128]{2,1,0:T(1,128)}), f32[128,1,128]{2,1,0:T(1,128)S(1)}, u32[]{:S(2)}, u32[]{:S(2)}) async-start(f32[128,1,128]{2,1,0:T(1,128)} %reshape.337), calls=%async_computation | async-start | bytes 131072 | tf_op jit(solution)/shard_map/while/body/eval_jaxpr/all_to_all | solution.py:103
  133.7 3.5 collective-permute-start
  143.7 4.0 collective-permute-start.4
  165.7 4.6 fusion.207
  170.5 4.1 fusion.203
  180.0 11.9 %all-to-all-start = ((f32[128,1,128]{2,1,0:T(1,128)}), f32[128,1,128]{2,1,0:T(1,128)S(1)}, u32[]{:S(2)}, u32[]{:S(2)}) async-start(f32[128,1,128]{2,1,0:T(1,128)} %reshape.337), calls=%async_computation | async-start | bytes 131072 | tf_op jit(solution)/shard_map/while/body/eval_jaxpr/all_to_all | solution.py:103
  191.9 3.5 collective-permute-start
  201.9 4.0 collective-permute-start.4
  223.9 4.6 fusion.207
  228.7 4.1 fusion.203
  238.3 11.9 %all-to-all-start = ((f32[128,1,128]{2,1,0:T(1,128)}), f32[128,1,128]{2,1,0:T(1,128)S(1)}, u32[]{:S(2)}, u32[]{:S(2)}) async-start(f32[128,1,128]{2,1,0:T(1,128)} %reshape.337), calls=%async_computation | async-start | bytes 131072 | tf_op jit(solution)/shard_map/while/body/eval_jaxpr/all_to_all | solution.py:103
  250.2 3.5 collective-permute-start
  260.1 4.0 collective-permute-start.4
  282.1 4.6 fusion.207
  286.9 4.1 fusion.203
  296.5 11.9 %all-to-all-start = ((f32[128,1,128]{2,1,0:T(1,128)}), f32[128,1,128]{2,1,0:T(1,128)S(1)}, u32[]{:S(2)}, u32[]{:S(2)}) async-start(f32[128,1,128]{2,1,0:T(1,128)} %reshape.337), calls=%async_computation | async-start | bytes 131072 | tf_op jit(solution)/shard_map/while/body/eval_jaxpr/all_to_all | solution.py:103
  318.3 4.0 collective-permute-start.4
  340.3 4.6 fusion.207
  345.1 4.1 fusion.203
  354.7 11.9 %all-to-all-start = ((f32[128,1,128]{2,1,0:T(1,128)}), f32[128,1,128]{2,1,0:T(1,128)S(1)}, u32[]{:S(2)}, u32[]{:S(2)}) async-start(f32[128,1,128]{2,1,0:T(1,128)} %reshape.337), calls=%async_computation | async-start | bytes 131072 | tf_op jit(solution)/shard_map/while/body/eval_jaxpr/all_to_all | solution.py:103
  376.6 4.0 collective-permute-start.4
  398.6 4.6 fusion.207
  403.3 4.1 fusion.203
  412.9 11.9 %all-to-all-start = ((f32[128,1,128]{2,1,0:T(1,128)}), f32[128,1,128]{2,1,0:T(1,128)S(1)}, u32[]{:S(2)}, u32[]{:S(2)}) async-start(f32[128,1,128]{2,1,0:T(1,128)} %reshape.337), calls=%async_computation | async-start | bytes 131072 | tf_op jit(solution)/shard_map/while/body/eval_jaxpr/all_to_all | solution.py:103
  434.8 4.0 collective-permute-start.4
  456.8 4.6 fusion.207
  461.5 4.1 fusion.203
  471.1 11.9 %all-to-all-start = ((f32[128,1,128]{2,1,0:T(1,128)}), f32[128,1,128]{2,1,0:T(1,128)S(1)}, u32[]{:S(2)}, u32[]{:S(2)}) async-start(f32[128,1,128]{2,1,0:T(1,128)} %reshape.337), calls=%async_computation | async-start | bytes 131072 | tf_op jit(solution)/shard_map/while/body/eval_jaxpr/all_to_all | solution.py:103
  493.0 4.0 collective-permute-start.4
  515.0 4.6 fusion.207
  519.8 4.1 fusion.203
  529.3 11.9 %all-to-all-start = ((f32[128,1,128]{2,1,0:T(1,128)}), f32[128,1,128]{2,1,0:T(1,128)S(1)}, u32[]{:S(2)}, u32[]{:S(2)}) async-start(f32[128,1,128]{2,1,0:T(1,128)} %reshape.337), calls=%async_computation | async-start | bytes 131072 | tf_op jit(solution)/shard_map/while/body/eval_jaxpr/all_to_all | solution.py:103
  551.2 4.0 collective-permute-start.4
  573.2 4.6 fusion.207
  578.0 4.1 fusion.203
  587.5 11.9 %all-to-all-start = ((f32[128,1,128]{2,1,0:T(1,128)}), f32[128,1,128]{2,1,0:T(1,128)S(1)}, u32[]{:S(2)}, u32[]{:S(2)}) async-start(f32[128,1,128]{2,1,0:T(1,128)} %reshape.337), calls=%async_computation | async-start | bytes 131072 | tf_op jit(solution)/shard_map/while/body/eval_jaxpr/all_to_all | solution.py:103
  609.4 4.0 collective-permute-start.4
  631.4 4.6 fusion.207
  636.2 4.1 fusion.203
  645.8 11.9 %all-to-all-start = ((f32[128,1,128]{2,1,0:T(1,128)}), f32[128,1,128]{2,1,0:T(1,128)S(1)}, u32[]{:S(2)}, u32[]{:S(2)}) async-start(f32[128,1,128]{2,1,0:T(1,128)} %reshape.337), calls=%async_computation | async-start | bytes 131072 | tf_op jit(solution)/shard_map/while/body/eval_jaxpr/all_to_all | solution.py:103
  667.6 4.0 collective-permute-start.4
  689.6 4.6 fusion.207
  694.4 4.1 fusion.203
  704.0 11.9 %all-to-all-start = ((f32[128,1,128]{2,1,0:T(1,128)}), f32[128,1,128]{2,1,0:T(1,128)S(1)}, u32[]{:S(2)}, u32[]{:S(2)}) async-start(f32[128,1,128]{2,1,0:T(1,128)} %reshape.337), calls=%async_computation | async-start | bytes 131072 | tf_op jit(solution)/shard_map/while/body/eval_jaxpr/all_to_all | solution.py:103
  725.8 4.0 collective-permute-start.4
  747.8 4.6 fusion.207
  752.6 4.1 fusion.203
  762.2 11.9 %all-to-all-start = ((f32[128,1,128]{2,1,0:T(1,128)}), f32[128,1,128]{2,1,0:T(1,128)S(1)}, u32[]{:S(2)}, u32[]{:S(2)}) async-start(f32[128,1,128]{2,1,0:T(1,128)} %reshape.337), calls=%async_computation | async-start | bytes 131072 | tf_op jit(solution)/shard_map/while/body/eval_jaxpr/all_to_all | solution.py:103
  784.1 4.0 collective-permute-start.4
  806.1 4.6 fusion.207
  810.8 4.1 fusion.203
  820.4 11.9 %all-to-all-start = ((f32[128,1,128]{2,1,0:T(1,128)}), f32[128,1,128]{2,1,0:T(1,128)S(1)}, u32[]{:S(2)}, u32[]{:S(2)}) async-start(f32[128,1,128]{2,1,0:T(1,128)} %reshape.337), calls=%async_computation | async-start | bytes 131072 | tf_op jit(solution)/shard_map/while/body/eval_jaxpr/all_to_all | solution.py:103
  842.3 4.0 collective-permute-start.4
  864.3 4.6 fusion.207
  (732 shorter events, 464.3 us)
Async XLA Ops:
  71.2 28.2 %all-to-all-start = ((f32[128,1,128]{2,1,0:T(1,128)}), f32[128,1,128]{2,1,0:T(1,128)S(1)}, u32[]{:S(2)}, u32[]{:S(2)}) async-start(f32[128,1,128]{2,1,0:T(1,128)} %reshape.337), calls=%async_computation | async-start | bytes 131072 | tf_op jit(solution)/shard_map/while/body/eval_jaxpr/all_to_all | solution.py:103
  75.5 22.5 %collective-permute-start = (f32[1,16,128]{2,1,0:T(8,128)S(1)}, f32[1,16,128]{2,1,0:T(8,128)S(1)}, u32[]{:S(2)}, u32[]{:S(2)}) collective-permute-start(f32[1,16,128]{2,1,0:T(8,128)S(1)} %get-tuple-element.534), channel_id=1, source_target_pairs={{0,4},{4,8},{8,12},{12,16},{16,20},{20,24},{24,28},{28,32},{32,36}... | collective-permute-start | bytes 24584 | tf_op jit(solution)/shard_map/while/body/eval_jaxpr/ppermute | solution.py:21
  81.0 31.1 %collective-permute-start.2 = (f32[4,1,128]{2,1,0:T(1,128)S(1)}, f32[4,1,128]{2,1,0:T(1,128)S(1)}, u32[]{:S(2)}, u32[]{:S(2)}) collective-permute-start(f32[4,1,128]{2,1,0:T(1,128)S(1)} %get-tuple-element.536), channel_id=1, source_target_pairs={{0,1},{1,2},{2,3},{4,5},{5,6},{6,7},{8,9},{9,10},{10,11},{12,13},{... | collective-permute-start | bytes 6152 | tf_op jit(solution)/shard_map/while/body/eval_jaxpr/ppermute | solution.py:21
  84.1 28.0 %collective-permute-start.3 = (f32[4,1,128]{2,1,0:T(1,128)S(1)}, f32[4,1,128]{2,1,0:T(1,128)S(1)}, u32[]{:S(2)}, u32[]{:S(2)}) collective-permute-start(f32[4,1,128]{2,1,0:T(1,128)S(1)} %get-tuple-element.537), channel_id=1, source_target_pairs={{1,0},{2,1},{3,2},{5,4},{6,5},{7,6},{9,8},{10,9},{11,10},{13,12},{... | collective-permute-start | bytes 6152 | tf_op jit(solution)/shard_map/while/body/eval_jaxpr/ppermute | solution.py:22
  85.5 21.9 %collective-permute-start.4 = (f32[16,1]{1,0:T(8,128)S(1)}, f32[16,1]{1,0:T(8,128)S(1)}, u32[]{:S(2)}, u32[]{:S(2)}) collective-permute-start(f32[16,1]{1,0:T(8,128)S(1)} %get-tuple-element.541), channel_id=1, source_target_pairs={{0,1},{1,2},{2,3},{4,5},{5,6},{6,7},{8,9},{9,10},{10,11},{12,13},{... | collective-permute-start | bytes 200 | tf_op jit(solution)/shard_map/while/body/eval_jaxpr/ppermute | solution.py:38
  121.8 35.8 %all-to-all-start = ((f32[128,1,128]{2,1,0:T(1,128)}), f32[128,1,128]{2,1,0:T(1,128)S(1)}, u32[]{:S(2)}, u32[]{:S(2)}) async-start(f32[128,1,128]{2,1,0:T(1,128)} %reshape.337), calls=%async_computation | async-start | bytes 131072 | tf_op jit(solution)/shard_map/while/body/eval_jaxpr/all_to_all | solution.py:103
  133.7 22.5 %collective-permute-start = (f32[1,16,128]{2,1,0:T(8,128)S(1)}, f32[1,16,128]{2,1,0:T(8,128)S(1)}, u32[]{:S(2)}, u32[]{:S(2)}) collective-permute-start(f32[1,16,128]{2,1,0:T(8,128)S(1)} %get-tuple-element.534), channel_id=1, source_target_pairs={{0,4},{4,8},{8,12},{12,16},{16,20},{20,24},{24,28},{28,32},{32,36}... | collective-permute-start | bytes 24584 | tf_op jit(solution)/shard_map/while/body/eval_jaxpr/ppermute | solution.py:21
  139.2 31.1 %collective-permute-start.2 = (f32[4,1,128]{2,1,0:T(1,128)S(1)}, f32[4,1,128]{2,1,0:T(1,128)S(1)}, u32[]{:S(2)}, u32[]{:S(2)}) collective-permute-start(f32[4,1,128]{2,1,0:T(1,128)S(1)} %get-tuple-element.536), channel_id=1, source_target_pairs={{0,1},{1,2},{2,3},{4,5},{5,6},{6,7},{8,9},{9,10},{10,11},{12,13},{... | collective-permute-start | bytes 6152 | tf_op jit(solution)/shard_map/while/body/eval_jaxpr/ppermute | solution.py:21
  142.3 28.0 %collective-permute-start.3 = (f32[4,1,128]{2,1,0:T(1,128)S(1)}, f32[4,1,128]{2,1,0:T(1,128)S(1)}, u32[]{:S(2)}, u32[]{:S(2)}) collective-permute-start(f32[4,1,128]{2,1,0:T(1,128)S(1)} %get-tuple-element.537), channel_id=1, source_target_pairs={{1,0},{2,1},{3,2},{5,4},{6,5},{7,6},{9,8},{10,9},{11,10},{13,12},{... | collective-permute-start | bytes 6152 | tf_op jit(solution)/shard_map/while/body/eval_jaxpr/ppermute | solution.py:22
  143.7 21.9 %collective-permute-start.4 = (f32[16,1]{1,0:T(8,128)S(1)}, f32[16,1]{1,0:T(8,128)S(1)}, u32[]{:S(2)}, u32[]{:S(2)}) collective-permute-start(f32[16,1]{1,0:T(8,128)S(1)} %get-tuple-element.541), channel_id=1, source_target_pairs={{0,1},{1,2},{2,3},{4,5},{5,6},{6,7},{8,9},{9,10},{10,11},{12,13},{... | collective-permute-start | bytes 200 | tf_op jit(solution)/shard_map/while/body/eval_jaxpr/ppermute | solution.py:38
  180.0 35.8 %all-to-all-start = ((f32[128,1,128]{2,1,0:T(1,128)}), f32[128,1,128]{2,1,0:T(1,128)S(1)}, u32[]{:S(2)}, u32[]{:S(2)}) async-start(f32[128,1,128]{2,1,0:T(1,128)} %reshape.337), calls=%async_computation | async-start | bytes 131072 | tf_op jit(solution)/shard_map/while/body/eval_jaxpr/all_to_all | solution.py:103
  191.9 22.5 %collective-permute-start = (f32[1,16,128]{2,1,0:T(8,128)S(1)}, f32[1,16,128]{2,1,0:T(8,128)S(1)}, u32[]{:S(2)}, u32[]{:S(2)}) collective-permute-start(f32[1,16,128]{2,1,0:T(8,128)S(1)} %get-tuple-element.534), channel_id=1, source_target_pairs={{0,4},{4,8},{8,12},{12,16},{16,20},{20,24},{24,28},{28,32},{32,36}... | collective-permute-start | bytes 24584 | tf_op jit(solution)/shard_map/while/body/eval_jaxpr/ppermute | solution.py:21
  197.4 31.1 %collective-permute-start.2 = (f32[4,1,128]{2,1,0:T(1,128)S(1)}, f32[4,1,128]{2,1,0:T(1,128)S(1)}, u32[]{:S(2)}, u32[]{:S(2)}) collective-permute-start(f32[4,1,128]{2,1,0:T(1,128)S(1)} %get-tuple-element.536), channel_id=1, source_target_pairs={{0,1},{1,2},{2,3},{4,5},{5,6},{6,7},{8,9},{9,10},{10,11},{12,13},{... | collective-permute-start | bytes 6152 | tf_op jit(solution)/shard_map/while/body/eval_jaxpr/ppermute | solution.py:21
  200.5 28.0 %collective-permute-start.3 = (f32[4,1,128]{2,1,0:T(1,128)S(1)}, f32[4,1,128]{2,1,0:T(1,128)S(1)}, u32[]{:S(2)}, u32[]{:S(2)}) collective-permute-start(f32[4,1,128]{2,1,0:T(1,128)S(1)} %get-tuple-element.537), channel_id=1, source_target_pairs={{1,0},{2,1},{3,2},{5,4},{6,5},{7,6},{9,8},{10,9},{11,10},{13,12},{... | collective-permute-start | bytes 6152 | tf_op jit(solution)/shard_map/while/body/eval_jaxpr/ppermute | solution.py:22
  201.9 21.9 %collective-permute-start.4 = (f32[16,1]{1,0:T(8,128)S(1)}, f32[16,1]{1,0:T(8,128)S(1)}, u32[]{:S(2)}, u32[]{:S(2)}) collective-permute-start(f32[16,1]{1,0:T(8,128)S(1)} %get-tuple-element.541), channel_id=1, source_target_pairs={{0,1},{1,2},{2,3},{4,5},{5,6},{6,7},{8,9},{9,10},{10,11},{12,13},{... | collective-permute-start | bytes 200 | tf_op jit(solution)/shard_map/while/body/eval_jaxpr/ppermute | solution.py:38
  238.3 35.8 %all-to-all-start = ((f32[128,1,128]{2,1,0:T(1,128)}), f32[128,1,128]{2,1,0:T(1,128)S(1)}, u32[]{:S(2)}, u32[]{:S(2)}) async-start(f32[128,1,128]{2,1,0:T(1,128)} %reshape.337), calls=%async_computation | async-start | bytes 131072 | tf_op jit(solution)/shard_map/while/body/eval_jaxpr/all_to_all | solution.py:103
  250.2 22.5 %collective-permute-start = (f32[1,16,128]{2,1,0:T(8,128)S(1)}, f32[1,16,128]{2,1,0:T(8,128)S(1)}, u32[]{:S(2)}, u32[]{:S(2)}) collective-permute-start(f32[1,16,128]{2,1,0:T(8,128)S(1)} %get-tuple-element.534), channel_id=1, source_target_pairs={{0,4},{4,8},{8,12},{12,16},{16,20},{20,24},{24,28},{28,32},{32,36}... | collective-permute-start | bytes 24584 | tf_op jit(solution)/shard_map/while/body/eval_jaxpr/ppermute | solution.py:21
  255.7 31.1 %collective-permute-start.2 = (f32[4,1,128]{2,1,0:T(1,128)S(1)}, f32[4,1,128]{2,1,0:T(1,128)S(1)}, u32[]{:S(2)}, u32[]{:S(2)}) collective-permute-start(f32[4,1,128]{2,1,0:T(1,128)S(1)} %get-tuple-element.536), channel_id=1, source_target_pairs={{0,1},{1,2},{2,3},{4,5},{5,6},{6,7},{8,9},{9,10},{10,11},{12,13},{... | collective-permute-start | bytes 6152 | tf_op jit(solution)/shard_map/while/body/eval_jaxpr/ppermute | solution.py:21
  258.7 28.0 %collective-permute-start.3 = (f32[4,1,128]{2,1,0:T(1,128)S(1)}, f32[4,1,128]{2,1,0:T(1,128)S(1)}, u32[]{:S(2)}, u32[]{:S(2)}) collective-permute-start(f32[4,1,128]{2,1,0:T(1,128)S(1)} %get-tuple-element.537), channel_id=1, source_target_pairs={{1,0},{2,1},{3,2},{5,4},{6,5},{7,6},{9,8},{10,9},{11,10},{13,12},{... | collective-permute-start | bytes 6152 | tf_op jit(solution)/shard_map/while/body/eval_jaxpr/ppermute | solution.py:22
  260.1 21.9 %collective-permute-start.4 = (f32[16,1]{1,0:T(8,128)S(1)}, f32[16,1]{1,0:T(8,128)S(1)}, u32[]{:S(2)}, u32[]{:S(2)}) collective-permute-start(f32[16,1]{1,0:T(8,128)S(1)} %get-tuple-element.541), channel_id=1, source_target_pairs={{0,1},{1,2},{2,3},{4,5},{5,6},{6,7},{8,9},{9,10},{10,11},{12,13},{... | collective-permute-start | bytes 200 | tf_op jit(solution)/shard_map/while/body/eval_jaxpr/ppermute | solution.py:38
  296.5 35.8 %all-to-all-start = ((f32[128,1,128]{2,1,0:T(1,128)}), f32[128,1,128]{2,1,0:T(1,128)S(1)}, u32[]{:S(2)}, u32[]{:S(2)}) async-start(f32[128,1,128]{2,1,0:T(1,128)} %reshape.337), calls=%async_computation | async-start | bytes 131072 | tf_op jit(solution)/shard_map/while/body/eval_jaxpr/all_to_all | solution.py:103
  308.4 22.5 %collective-permute-start = (f32[1,16,128]{2,1,0:T(8,128)S(1)}, f32[1,16,128]{2,1,0:T(8,128)S(1)}, u32[]{:S(2)}, u32[]{:S(2)}) collective-permute-start(f32[1,16,128]{2,1,0:T(8,128)S(1)} %get-tuple-element.534), channel_id=1, source_target_pairs={{0,4},{4,8},{8,12},{12,16},{16,20},{20,24},{24,28},{28,32},{32,36}... | collective-permute-start | bytes 24584 | tf_op jit(solution)/shard_map/while/body/eval_jaxpr/ppermute | solution.py:21
  313.9 31.1 %collective-permute-start.2 = (f32[4,1,128]{2,1,0:T(1,128)S(1)}, f32[4,1,128]{2,1,0:T(1,128)S(1)}, u32[]{:S(2)}, u32[]{:S(2)}) collective-permute-start(f32[4,1,128]{2,1,0:T(1,128)S(1)} %get-tuple-element.536), channel_id=1, source_target_pairs={{0,1},{1,2},{2,3},{4,5},{5,6},{6,7},{8,9},{9,10},{10,11},{12,13},{... | collective-permute-start | bytes 6152 | tf_op jit(solution)/shard_map/while/body/eval_jaxpr/ppermute | solution.py:21
  317.0 28.0 %collective-permute-start.3 = (f32[4,1,128]{2,1,0:T(1,128)S(1)}, f32[4,1,128]{2,1,0:T(1,128)S(1)}, u32[]{:S(2)}, u32[]{:S(2)}) collective-permute-start(f32[4,1,128]{2,1,0:T(1,128)S(1)} %get-tuple-element.537), channel_id=1, source_target_pairs={{1,0},{2,1},{3,2},{5,4},{6,5},{7,6},{9,8},{10,9},{11,10},{13,12},{... | collective-permute-start | bytes 6152 | tf_op jit(solution)/shard_map/while/body/eval_jaxpr/ppermute | solution.py:22
  318.3 21.9 %collective-permute-start.4 = (f32[16,1]{1,0:T(8,128)S(1)}, f32[16,1]{1,0:T(8,128)S(1)}, u32[]{:S(2)}, u32[]{:S(2)}) collective-permute-start(f32[16,1]{1,0:T(8,128)S(1)} %get-tuple-element.541), channel_id=1, source_target_pairs={{0,1},{1,2},{2,3},{4,5},{5,6},{6,7},{8,9},{9,10},{10,11},{12,13},{... | collective-permute-start | bytes 200 | tf_op jit(solution)/shard_map/while/body/eval_jaxpr/ppermute | solution.py:38
  354.7 35.8 %all-to-all-start = ((f32[128,1,128]{2,1,0:T(1,128)}), f32[128,1,128]{2,1,0:T(1,128)S(1)}, u32[]{:S(2)}, u32[]{:S(2)}) async-start(f32[128,1,128]{2,1,0:T(1,128)} %reshape.337), calls=%async_computation | async-start | bytes 131072 | tf_op jit(solution)/shard_map/while/body/eval_jaxpr/all_to_all | solution.py:103
  366.6 22.5 %collective-permute-start = (f32[1,16,128]{2,1,0:T(8,128)S(1)}, f32[1,16,128]{2,1,0:T(8,128)S(1)}, u32[]{:S(2)}, u32[]{:S(2)}) collective-permute-start(f32[1,16,128]{2,1,0:T(8,128)S(1)} %get-tuple-element.534), channel_id=1, source_target_pairs={{0,4},{4,8},{8,12},{12,16},{16,20},{20,24},{24,28},{28,32},{32,36}... | collective-permute-start | bytes 24584 | tf_op jit(solution)/shard_map/while/body/eval_jaxpr/ppermute | solution.py:21
  372.1 31.1 %collective-permute-start.2 = (f32[4,1,128]{2,1,0:T(1,128)S(1)}, f32[4,1,128]{2,1,0:T(1,128)S(1)}, u32[]{:S(2)}, u32[]{:S(2)}) collective-permute-start(f32[4,1,128]{2,1,0:T(1,128)S(1)} %get-tuple-element.536), channel_id=1, source_target_pairs={{0,1},{1,2},{2,3},{4,5},{5,6},{6,7},{8,9},{9,10},{10,11},{12,13},{... | collective-permute-start | bytes 6152 | tf_op jit(solution)/shard_map/while/body/eval_jaxpr/ppermute | solution.py:21
  375.2 28.0 %collective-permute-start.3 = (f32[4,1,128]{2,1,0:T(1,128)S(1)}, f32[4,1,128]{2,1,0:T(1,128)S(1)}, u32[]{:S(2)}, u32[]{:S(2)}) collective-permute-start(f32[4,1,128]{2,1,0:T(1,128)S(1)} %get-tuple-element.537), channel_id=1, source_target_pairs={{1,0},{2,1},{3,2},{5,4},{6,5},{7,6},{9,8},{10,9},{11,10},{13,12},{... | collective-permute-start | bytes 6152 | tf_op jit(solution)/shard_map/while/body/eval_jaxpr/ppermute | solution.py:22
  376.6 21.9 %collective-permute-start.4 = (f32[16,1]{1,0:T(8,128)S(1)}, f32[16,1]{1,0:T(8,128)S(1)}, u32[]{:S(2)}, u32[]{:S(2)}) collective-permute-start(f32[16,1]{1,0:T(8,128)S(1)} %get-tuple-element.541), channel_id=1, source_target_pairs={{0,1},{1,2},{2,3},{4,5},{5,6},{6,7},{8,9},{9,10},{10,11},{12,13},{... | collective-permute-start | bytes 200 | tf_op jit(solution)/shard_map/while/body/eval_jaxpr/ppermute | solution.py:38
  412.9 35.8 %all-to-all-start = ((f32[128,1,128]{2,1,0:T(1,128)}), f32[128,1,128]{2,1,0:T(1,128)S(1)}, u32[]{:S(2)}, u32[]{:S(2)}) async-start(f32[128,1,128]{2,1,0:T(1,128)} %reshape.337), calls=%async_computation | async-start | bytes 131072 | tf_op jit(solution)/shard_map/while/body/eval_jaxpr/all_to_all | solution.py:103
  424.8 22.5 %collective-permute-start = (f32[1,16,128]{2,1,0:T(8,128)S(1)}, f32[1,16,128]{2,1,0:T(8,128)S(1)}, u32[]{:S(2)}, u32[]{:S(2)}) collective-permute-start(f32[1,16,128]{2,1,0:T(8,128)S(1)} %get-tuple-element.534), channel_id=1, source_target_pairs={{0,4},{4,8},{8,12},{12,16},{16,20},{20,24},{24,28},{28,32},{32,36}... | collective-permute-start | bytes 24584 | tf_op jit(solution)/shard_map/while/body/eval_jaxpr/ppermute | solution.py:21
  430.3 31.1 %collective-permute-start.2 = (f32[4,1,128]{2,1,0:T(1,128)S(1)}, f32[4,1,128]{2,1,0:T(1,128)S(1)}, u32[]{:S(2)}, u32[]{:S(2)}) collective-permute-start(f32[4,1,128]{2,1,0:T(1,128)S(1)} %get-tuple-element.536), channel_id=1, source_target_pairs={{0,1},{1,2},{2,3},{4,5},{5,6},{6,7},{8,9},{9,10},{10,11},{12,13},{... | collective-permute-start | bytes 6152 | tf_op jit(solution)/shard_map/while/body/eval_jaxpr/ppermute | solution.py:21
  433.4 28.0 %collective-permute-start.3 = (f32[4,1,128]{2,1,0:T(1,128)S(1)}, f32[4,1,128]{2,1,0:T(1,128)S(1)}, u32[]{:S(2)}, u32[]{:S(2)}) collective-permute-start(f32[4,1,128]{2,1,0:T(1,128)S(1)} %get-tuple-element.537), channel_id=1, source_target_pairs={{1,0},{2,1},{3,2},{5,4},{6,5},{7,6},{9,8},{10,9},{11,10},{13,12},{... | collective-permute-start | bytes 6152 | tf_op jit(solution)/shard_map/while/body/eval_jaxpr/ppermute | solution.py:22
  434.8 21.9 %collective-permute-start.4 = (f32[16,1]{1,0:T(8,128)S(1)}, f32[16,1]{1,0:T(8,128)S(1)}, u32[]{:S(2)}, u32[]{:S(2)}) collective-permute-start(f32[16,1]{1,0:T(8,128)S(1)} %get-tuple-element.541), channel_id=1, source_target_pairs={{0,1},{1,2},{2,3},{4,5},{5,6},{6,7},{8,9},{9,10},{10,11},{12,13},{... | collective-permute-start | bytes 200 | tf_op jit(solution)/shard_map/while/body/eval_jaxpr/ppermute | solution.py:38
  471.1 35.8 %all-to-all-start = ((f32[128,1,128]{2,1,0:T(1,128)}), f32[128,1,128]{2,1,0:T(1,128)S(1)}, u32[]{:S(2)}, u32[]{:S(2)}) async-start(f32[128,1,128]{2,1,0:T(1,128)} %reshape.337), calls=%async_computation | async-start | bytes 131072 | tf_op jit(solution)/shard_map/while/body/eval_jaxpr/all_to_all | solution.py:103
  483.0 22.5 %collective-permute-start = (f32[1,16,128]{2,1,0:T(8,128)S(1)}, f32[1,16,128]{2,1,0:T(8,128)S(1)}, u32[]{:S(2)}, u32[]{:S(2)}) collective-permute-start(f32[1,16,128]{2,1,0:T(8,128)S(1)} %get-tuple-element.534), channel_id=1, source_target_pairs={{0,4},{4,8},{8,12},{12,16},{16,20},{20,24},{24,28},{28,32},{32,36}... | collective-permute-start | bytes 24584 | tf_op jit(solution)/shard_map/while/body/eval_jaxpr/ppermute | solution.py:21
  488.5 31.1 %collective-permute-start.2 = (f32[4,1,128]{2,1,0:T(1,128)S(1)}, f32[4,1,128]{2,1,0:T(1,128)S(1)}, u32[]{:S(2)}, u32[]{:S(2)}) collective-permute-start(f32[4,1,128]{2,1,0:T(1,128)S(1)} %get-tuple-element.536), channel_id=1, source_target_pairs={{0,1},{1,2},{2,3},{4,5},{5,6},{6,7},{8,9},{9,10},{10,11},{12,13},{... | collective-permute-start | bytes 6152 | tf_op jit(solution)/shard_map/while/body/eval_jaxpr/ppermute | solution.py:21
  491.6 28.0 %collective-permute-start.3 = (f32[4,1,128]{2,1,0:T(1,128)S(1)}, f32[4,1,128]{2,1,0:T(1,128)S(1)}, u32[]{:S(2)}, u32[]{:S(2)}) collective-permute-start(f32[4,1,128]{2,1,0:T(1,128)S(1)} %get-tuple-element.537), channel_id=1, source_target_pairs={{1,0},{2,1},{3,2},{5,4},{6,5},{7,6},{9,8},{10,9},{11,10},{13,12},{... | collective-permute-start | bytes 6152 | tf_op jit(solution)/shard_map/while/body/eval_jaxpr/ppermute | solution.py:22
  493.0 21.9 %collective-permute-start.4 = (f32[16,1]{1,0:T(8,128)S(1)}, f32[16,1]{1,0:T(8,128)S(1)}, u32[]{:S(2)}, u32[]{:S(2)}) collective-permute-start(f32[16,1]{1,0:T(8,128)S(1)} %get-tuple-element.541), channel_id=1, source_target_pairs={{0,1},{1,2},{2,3},{4,5},{5,6},{6,7},{8,9},{9,10},{10,11},{12,13},{... | collective-permute-start | bytes 200 | tf_op jit(solution)/shard_map/while/body/eval_jaxpr/ppermute | solution.py:38
  529.3 35.8 %all-to-all-start = ((f32[128,1,128]{2,1,0:T(1,128)}), f32[128,1,128]{2,1,0:T(1,128)S(1)}, u32[]{:S(2)}, u32[]{:S(2)}) async-start(f32[128,1,128]{2,1,0:T(1,128)} %reshape.337), calls=%async_computation | async-start | bytes 131072 | tf_op jit(solution)/shard_map/while/body/eval_jaxpr/all_to_all | solution.py:103
  541.2 22.5 %collective-permute-start = (f32[1,16,128]{2,1,0:T(8,128)S(1)}, f32[1,16,128]{2,1,0:T(8,128)S(1)}, u32[]{:S(2)}, u32[]{:S(2)}) collective-permute-start(f32[1,16,128]{2,1,0:T(8,128)S(1)} %get-tuple-element.534), channel_id=1, source_target_pairs={{0,4},{4,8},{8,12},{12,16},{16,20},{20,24},{24,28},{28,32},{32,36}... | collective-permute-start | bytes 24584 | tf_op jit(solution)/shard_map/while/body/eval_jaxpr/ppermute | solution.py:21
  546.7 31.1 %collective-permute-start.2 = (f32[4,1,128]{2,1,0:T(1,128)S(1)}, f32[4,1,128]{2,1,0:T(1,128)S(1)}, u32[]{:S(2)}, u32[]{:S(2)}) collective-permute-start(f32[4,1,128]{2,1,0:T(1,128)S(1)} %get-tuple-element.536), channel_id=1, source_target_pairs={{0,1},{1,2},{2,3},{4,5},{5,6},{6,7},{8,9},{9,10},{10,11},{12,13},{... | collective-permute-start | bytes 6152 | tf_op jit(solution)/shard_map/while/body/eval_jaxpr/ppermute | solution.py:21
  549.8 28.0 %collective-permute-start.3 = (f32[4,1,128]{2,1,0:T(1,128)S(1)}, f32[4,1,128]{2,1,0:T(1,128)S(1)}, u32[]{:S(2)}, u32[]{:S(2)}) collective-permute-start(f32[4,1,128]{2,1,0:T(1,128)S(1)} %get-tuple-element.537), channel_id=1, source_target_pairs={{1,0},{2,1},{3,2},{5,4},{6,5},{7,6},{9,8},{10,9},{11,10},{13,12},{... | collective-permute-start | bytes 6152 | tf_op jit(solution)/shard_map/while/body/eval_jaxpr/ppermute | solution.py:22
  587.5 35.8 %all-to-all-start = ((f32[128,1,128]{2,1,0:T(1,128)}), f32[128,1,128]{2,1,0:T(1,128)S(1)}, u32[]{:S(2)}, u32[]{:S(2)}) async-start(f32[128,1,128]{2,1,0:T(1,128)} %reshape.337), calls=%async_computation | async-start | bytes 131072 | tf_op jit(solution)/shard_map/while/body/eval_jaxpr/all_to_all | solution.py:103
  599.4 22.5 %collective-permute-start = (f32[1,16,128]{2,1,0:T(8,128)S(1)}, f32[1,16,128]{2,1,0:T(8,128)S(1)}, u32[]{:S(2)}, u32[]{:S(2)}) collective-permute-start(f32[1,16,128]{2,1,0:T(8,128)S(1)} %get-tuple-element.534), channel_id=1, source_target_pairs={{0,4},{4,8},{8,12},{12,16},{16,20},{20,24},{24,28},{28,32},{32,36}... | collective-permute-start | bytes 24584 | tf_op jit(solution)/shard_map/while/body/eval_jaxpr/ppermute | solution.py:21
  604.9 31.1 %collective-permute-start.2 = (f32[4,1,128]{2,1,0:T(1,128)S(1)}, f32[4,1,128]{2,1,0:T(1,128)S(1)}, u32[]{:S(2)}, u32[]{:S(2)}) collective-permute-start(f32[4,1,128]{2,1,0:T(1,128)S(1)} %get-tuple-element.536), channel_id=1, source_target_pairs={{0,1},{1,2},{2,3},{4,5},{5,6},{6,7},{8,9},{9,10},{10,11},{12,13},{... | collective-permute-start | bytes 6152 | tf_op jit(solution)/shard_map/while/body/eval_jaxpr/ppermute | solution.py:21
  608.0 28.0 %collective-permute-start.3 = (f32[4,1,128]{2,1,0:T(1,128)S(1)}, f32[4,1,128]{2,1,0:T(1,128)S(1)}, u32[]{:S(2)}, u32[]{:S(2)}) collective-permute-start(f32[4,1,128]{2,1,0:T(1,128)S(1)} %get-tuple-element.537), channel_id=1, source_target_pairs={{1,0},{2,1},{3,2},{5,4},{6,5},{7,6},{9,8},{10,9},{11,10},{13,12},{... | collective-permute-start | bytes 6152 | tf_op jit(solution)/shard_map/while/body/eval_jaxpr/ppermute | solution.py:22
  645.8 35.8 %all-to-all-start = ((f32[128,1,128]{2,1,0:T(1,128)}), f32[128,1,128]{2,1,0:T(1,128)S(1)}, u32[]{:S(2)}, u32[]{:S(2)}) async-start(f32[128,1,128]{2,1,0:T(1,128)} %reshape.337), calls=%async_computation | async-start | bytes 131072 | tf_op jit(solution)/shard_map/while/body/eval_jaxpr/all_to_all | solution.py:103
  657.7 22.5 %collective-permute-start = (f32[1,16,128]{2,1,0:T(8,128)S(1)}, f32[1,16,128]{2,1,0:T(8,128)S(1)}, u32[]{:S(2)}, u32[]{:S(2)}) collective-permute-start(f32[1,16,128]{2,1,0:T(8,128)S(1)} %get-tuple-element.534), channel_id=1, source_target_pairs={{0,4},{4,8},{8,12},{12,16},{16,20},{20,24},{24,28},{28,32},{32,36}... | collective-permute-start | bytes 24584 | tf_op jit(solution)/shard_map/while/body/eval_jaxpr/ppermute | solution.py:21
  663.2 31.1 %collective-permute-start.2 = (f32[4,1,128]{2,1,0:T(1,128)S(1)}, f32[4,1,128]{2,1,0:T(1,128)S(1)}, u32[]{:S(2)}, u32[]{:S(2)}) collective-permute-start(f32[4,1,128]{2,1,0:T(1,128)S(1)} %get-tuple-element.536), channel_id=1, source_target_pairs={{0,1},{1,2},{2,3},{4,5},{5,6},{6,7},{8,9},{9,10},{10,11},{12,13},{... | collective-permute-start | bytes 6152 | tf_op jit(solution)/shard_map/while/body/eval_jaxpr/ppermute | solution.py:21
  666.3 28.0 %collective-permute-start.3 = (f32[4,1,128]{2,1,0:T(1,128)S(1)}, f32[4,1,128]{2,1,0:T(1,128)S(1)}, u32[]{:S(2)}, u32[]{:S(2)}) collective-permute-start(f32[4,1,128]{2,1,0:T(1,128)S(1)} %get-tuple-element.537), channel_id=1, source_target_pairs={{1,0},{2,1},{3,2},{5,4},{6,5},{7,6},{9,8},{10,9},{11,10},{13,12},{... | collective-permute-start | bytes 6152 | tf_op jit(solution)/shard_map/while/body/eval_jaxpr/ppermute | solution.py:22
  704.0 35.8 %all-to-all-start = ((f32[128,1,128]{2,1,0:T(1,128)}), f32[128,1,128]{2,1,0:T(1,128)S(1)}, u32[]{:S(2)}, u32[]{:S(2)}) async-start(f32[128,1,128]{2,1,0:T(1,128)} %reshape.337), calls=%async_computation | async-start | bytes 131072 | tf_op jit(solution)/shard_map/while/body/eval_jaxpr/all_to_all | solution.py:103
  715.9 22.5 %collective-permute-start = (f32[1,16,128]{2,1,0:T(8,128)S(1)}, f32[1,16,128]{2,1,0:T(8,128)S(1)}, u32[]{:S(2)}, u32[]{:S(2)}) collective-permute-start(f32[1,16,128]{2,1,0:T(8,128)S(1)} %get-tuple-element.534), channel_id=1, source_target_pairs={{0,4},{4,8},{8,12},{12,16},{16,20},{20,24},{24,28},{28,32},{32,36}... | collective-permute-start | bytes 24584 | tf_op jit(solution)/shard_map/while/body/eval_jaxpr/ppermute | solution.py:21
  721.4 31.1 %collective-permute-start.2 = (f32[4,1,128]{2,1,0:T(1,128)S(1)}, f32[4,1,128]{2,1,0:T(1,128)S(1)}, u32[]{:S(2)}, u32[]{:S(2)}) collective-permute-start(f32[4,1,128]{2,1,0:T(1,128)S(1)} %get-tuple-element.536), channel_id=1, source_target_pairs={{0,1},{1,2},{2,3},{4,5},{5,6},{6,7},{8,9},{9,10},{10,11},{12,13},{... | collective-permute-start | bytes 6152 | tf_op jit(solution)/shard_map/while/body/eval_jaxpr/ppermute | solution.py:21
  724.5 28.0 %collective-permute-start.3 = (f32[4,1,128]{2,1,0:T(1,128)S(1)}, f32[4,1,128]{2,1,0:T(1,128)S(1)}, u32[]{:S(2)}, u32[]{:S(2)}) collective-permute-start(f32[4,1,128]{2,1,0:T(1,128)S(1)} %get-tuple-element.537), channel_id=1, source_target_pairs={{1,0},{2,1},{3,2},{5,4},{6,5},{7,6},{9,8},{10,9},{11,10},{13,12},{... | collective-permute-start | bytes 6152 | tf_op jit(solution)/shard_map/while/body/eval_jaxpr/ppermute | solution.py:22
  762.2 35.8 %all-to-all-start = ((f32[128,1,128]{2,1,0:T(1,128)}), f32[128,1,128]{2,1,0:T(1,128)S(1)}, u32[]{:S(2)}, u32[]{:S(2)}) async-start(f32[128,1,128]{2,1,0:T(1,128)} %reshape.337), calls=%async_computation | async-start | bytes 131072 | tf_op jit(solution)/shard_map/while/body/eval_jaxpr/all_to_all | solution.py:103
  774.1 22.5 %collective-permute-start = (f32[1,16,128]{2,1,0:T(8,128)S(1)}, f32[1,16,128]{2,1,0:T(8,128)S(1)}, u32[]{:S(2)}, u32[]{:S(2)}) collective-permute-start(f32[1,16,128]{2,1,0:T(8,128)S(1)} %get-tuple-element.534), channel_id=1, source_target_pairs={{0,4},{4,8},{8,12},{12,16},{16,20},{20,24},{24,28},{28,32},{32,36}... | collective-permute-start | bytes 24584 | tf_op jit(solution)/shard_map/while/body/eval_jaxpr/ppermute | solution.py:21
  779.6 31.1 %collective-permute-start.2 = (f32[4,1,128]{2,1,0:T(1,128)S(1)}, f32[4,1,128]{2,1,0:T(1,128)S(1)}, u32[]{:S(2)}, u32[]{:S(2)}) collective-permute-start(f32[4,1,128]{2,1,0:T(1,128)S(1)} %get-tuple-element.536), channel_id=1, source_target_pairs={{0,1},{1,2},{2,3},{4,5},{5,6},{6,7},{8,9},{9,10},{10,11},{12,13},{... | collective-permute-start | bytes 6152 | tf_op jit(solution)/shard_map/while/body/eval_jaxpr/ppermute | solution.py:21
  782.7 28.0 %collective-permute-start.3 = (f32[4,1,128]{2,1,0:T(1,128)S(1)}, f32[4,1,128]{2,1,0:T(1,128)S(1)}, u32[]{:S(2)}, u32[]{:S(2)}) collective-permute-start(f32[4,1,128]{2,1,0:T(1,128)S(1)} %get-tuple-element.537), channel_id=1, source_target_pairs={{1,0},{2,1},{3,2},{5,4},{6,5},{7,6},{9,8},{10,9},{11,10},{13,12},{... | collective-permute-start | bytes 6152 | tf_op jit(solution)/shard_map/while/body/eval_jaxpr/ppermute | solution.py:22
  820.4 35.8 %all-to-all-start = ((f32[128,1,128]{2,1,0:T(1,128)}), f32[128,1,128]{2,1,0:T(1,128)S(1)}, u32[]{:S(2)}, u32[]{:S(2)}) async-start(f32[128,1,128]{2,1,0:T(1,128)} %reshape.337), calls=%async_computation | async-start | bytes 131072 | tf_op jit(solution)/shard_map/while/body/eval_jaxpr/all_to_all | solution.py:103
  832.3 22.5 %collective-permute-start = (f32[1,16,128]{2,1,0:T(8,128)S(1)}, f32[1,16,128]{2,1,0:T(8,128)S(1)}, u32[]{:S(2)}, u32[]{:S(2)}) collective-permute-start(f32[1,16,128]{2,1,0:T(8,128)S(1)} %get-tuple-element.534), channel_id=1, source_target_pairs={{0,4},{4,8},{8,12},{12,16},{16,20},{20,24},{24,28},{28,32},{32,36}... | collective-permute-start | bytes 24584 | tf_op jit(solution)/shard_map/while/body/eval_jaxpr/ppermute | solution.py:21
  837.8 31.1 %collective-permute-start.2 = (f32[4,1,128]{2,1,0:T(1,128)S(1)}, f32[4,1,128]{2,1,0:T(1,128)S(1)}, u32[]{:S(2)}, u32[]{:S(2)}) collective-permute-start(f32[4,1,128]{2,1,0:T(1,128)S(1)} %get-tuple-element.536), channel_id=1, source_target_pairs={{0,1},{1,2},{2,3},{4,5},{5,6},{6,7},{8,9},{9,10},{10,11},{12,13},{... | collective-permute-start | bytes 6152 | tf_op jit(solution)/shard_map/while/body/eval_jaxpr/ppermute | solution.py:21
  840.9 28.0 %collective-permute-start.3 = (f32[4,1,128]{2,1,0:T(1,128)S(1)}, f32[4,1,128]{2,1,0:T(1,128)S(1)}, u32[]{:S(2)}, u32[]{:S(2)}) collective-permute-start(f32[4,1,128]{2,1,0:T(1,128)S(1)} %get-tuple-element.537), channel_id=1, source_target_pairs={{1,0},{2,1},{3,2},{5,4},{6,5},{7,6},{9,8},{10,9},{11,10},{13,12},{... | collective-permute-start | bytes 6152 | tf_op jit(solution)/shard_map/while/body/eval_jaxpr/ppermute | solution.py:22
  (52 other events, 1144.1 us)
where the time goes:
time: 876 us; the launch traced here: 870 us
  starting transfers between devices  382 us (44%)
  matrix products  354 us (40%)
  local copies, waits for them, and re-layouts  65.3 us (7%)
  other arithmetic  52.7 us (6%)
  waiting for transfers between devices  9.96 us (1%)
    all_to_all x14, starting transfers between devices, trade_both(): lax.all_to_all(paired, ('slab', 'plane'), split_axis=1, concat_axis=1, ti...  159 us
    dot_general x42, matrix products, place_values(): lax.dot_general(row_onehot, weighted, (((0,), (0,)), ((), ())), precision...  137 us
    dot_general x42, matrix products, pick_values(): jnp.dot(row_onehot, table, precision=lax.Precision.HIGHEST, preferred_ele...  132 us
    ppermute x28, starting transfers between devices, extended(): lax.ppermute(last, axis, up)  92.8 us
    ppermute x14, starting transfers between devices, with_halo(): lax.ppermute(lax.slice_in_dim(block, block.shape[dim] - width, None, axis...  55.7 us
    ppermute x28, starting transfers between devices, extended(): lax.ppermute(first, axis, [(b, a) for a, b in up])  45 us
    dot_general x28, matrix products, membrane(): jnp.tensordot(gate_cond * gate_rev, renewed, axes=1, precision=lax.Precis...  42.3 us
    dot_general x28, matrix products, membrane(): jnp.tensordot(gate_cond, renewed, axes=1, precision=lax.Precision.HIGHEST)  42.3 us
  transfers between devices with their start and end apart: 99, of which 1 were waited for; matrix products, arithmetic and copies ran while one was open for 34% of the time, Pallas kernels for 0%

commit v1 on v0

v1 whole, which is shorter than its diff:
```python
import functools

import jax
import jax.numpy as jnp
from jax import lax
from jax.experimental import pallas as pl
from jax.experimental.pallas import tpu as pltpu
from jax.sharding import PartitionSpec as P

STEPS = 14
DT = 0.1
LOG2E = 1.4426950408889634
MESH = pl.DeviceIdType.MESH
f32, bf16, i32 = jnp.float32, jnp.bfloat16, jnp.int32


def offsets():
    ring = lambda d: min(d, 4 - d)
    every = [(a, b, c, d) for a in range(4) for b in range(4) for c in range(2) for d in range(4)]
    far = lambda o: ring(o[0]) + ring(o[1]) + ring(o[3]) + 0.1 * o[2]
    return sorted([o for o in every if any(o)], key=lambda o: -far(o))


def iota(shape, dim):
    return lax.broadcasted_iota(i32, shape, dim)


def kernel(
    tv_ref, td_ref, fv_ref, fd_ref, tg_ref, fg_ref,
    half_ref, rate_ref, cond_ref, rev_ref, jcond_ref,
    jf_ref, jc_ref, jo_ref, jt_ref, jk_ref,
    to_ref, fo_ref,
    v_ref, d_ref, y_ref, prm_ref,
    oht_ref, kv_ref, rmask_ref, ct_ref, c_ref,
    row_ref, lane_ref, gain_ref, gsum_ref, graw_ref,
    s0_ref, r0_ref, s_ref, r_ref, hb_ref, hy_ref,
    gsem, s0sem, r0sem, ssem, rsem, hssem, hrsem,
):
    slab, plane = lax.axis_index("slab"), lax.axis_index("plane")
    me = slab * 4 + plane
    z, y, core = slab // 8, lax.rem(slab // 2, 4), lax.rem(slab, 2)
    half = me // 64
    q_me = lax.rem(me, 64)
    zs = [lax.rem(z + d, 4) * 8 for d in range(4)]
    ys = [lax.rem(y + d, 4) * 2 for d in range(4)]
    cs = [lax.rem(core + d, 2) for d in range(2)]
    xs = [lax.rem(plane + d, 4) for d in range(4)]
    peers = [(zs[a] + ys[b] + cs[c], xs[d]) for a, b, c, d in offsets()]

    loads = [pltpu.make_async_copy(tg_ref, y_ref.at[0], gsem.at[0])]
    for t in range(4):
        loads.append(pltpu.make_async_copy(fg_ref.at[:, :, pl.ds(t * 128, 128)], y_ref.at[1, :, t], gsem.at[1 + t]))
    for copy in loads:
        copy.start()

    barrier = pltpu.get_barrier_semaphore()

    def greet(k, carry):
        t = lax.rem(me + k, 128)
        pl.semaphore_signal(barrier, inc=1, device_id=(t // 4, lax.rem(t, 4)), device_id_type=MESH)
        return carry

    lax.fori_loop(1, 128, greet, 0)

    def params(k, carry):
        rate, cond = rate_ref[k], cond_ref[k]
        prm_ref[0, k] = 0.5 * half_ref[k]
        prm_ref[1, k] = rate * (-1.5 * DT * LOG2E)
        prm_ref[2, k] = rate * (-0.5 * DT * LOG2E)
        prm_ref[3, k] = 0.5 * cond
        prm_ref[4, k] = rev_ref[k]
        prm_ref[5, k] = cond
        return carry

    lax.fori_loop(0, 40, params, 0)

    v_ref[0, 0] = tv_ref[...]
    d_ref[0] = td_ref[...]
    for t in range(4):
        v_ref[1, 0, t] = fv_ref[:, t * 128:(t + 1) * 128]
        d_ref[1, t] = fd_ref[:, t * 128:(t + 1) * 128]

    sub = iota((128, 128), 0)
    sub64 = iota((64, 128), 0)
    lane = iota((128, 128), 1)
    lane64 = iota((64, 128), 1)
    before = jnp.concatenate([jnp.where(sub < lane, 1.0, 0.0), jnp.ones((128, 128), f32)], axis=1).astype(bf16)

    def chunk(c, count):
        at = pl.ds(c, 1)
        cols = pl.ds(pl.multiple_of(c * 128, 128), 128)
        hit = sub == jnp.broadcast_to(jo_ref[at, :], (128, 128))
        onehot = jnp.where(hit, 1.0, 0.0).astype(bf16)
        oht_ref[:, cols] = onehot
        seen = jnp.dot(onehot, before, preferred_element_type=f32)
        rank = jnp.sum(jnp.where(hit, seen[:, :128] + count, 0.0), axis=0, keepdims=True).astype(i32)
        place = sub64 == jnp.broadcast_to(rank, (64, 128))

        def put(p, value):
            value = jnp.broadcast_to(value.astype(f32), (64, 128))
            kv_ref[p * 64:(p + 1) * 64, cols] = jnp.where(place, value, 0.0).astype(bf16)

        cell, fcell = jt_ref[at, :], jc_ref[at, :]
        put(0, cell // 128)
        put(1, jk_ref[at, :] + 1)
        put(2, lax.rem(cell, 128))
        put(3, jnp.zeros_like(cell))
        put(4, (fcell // 128) * 16 + jf_ref[at, :])
        put(5, lax.rem(fcell, 128))
        return count + seen[:, 128:]

    lax.fori_loop(0, 32, chunk, jnp.zeros((128, 128), f32))
    slots = lax.dot_general(oht_ref[...], kv_ref[...], (((1,), (1,)), ((), ())), preferred_element_type=f32)
    first, second, third = slots[:, :128], slots[:, 128:256], slots[:, 256:]
    gain = jnp.zeros((128, 128), f32)
    for k in range(8):
        gain = jnp.where(first == float(k + 1), jcond_ref[k], gain)
    s0_ref[...] = jnp.where(lane < 64, first * 128.0 + second, gain)

    def turn(array):
        return pltpu.roll(array, 64, 1)

    def low_pair(array):
        return jnp.where(lane64 < 64, array[:64], turn(array[64:]))

    def high_pair(array):
        return jnp.where(lane64 < 64, turn(array[:64]), array[64:])

    row_ref[1] = low_pair(third).astype(i32)
    lane_ref[1] = high_pair(third).astype(i32)
    gain_ref[1] = high_pair(s0_ref[...])
    gain_ref[0] = jnp.ones((64, 128), f32)
    graw_ref[1] = gain_ref[1]

    pl.semaphore_wait(barrier, 127)

    own0 = pltpu.make_async_copy(s0_ref.at[pl.ds(me, 1)], r0_ref.at[pl.ds(me, 1)], r0sem)
    for ts, tp in peers:
        pltpu.make_async_remote_copy(
            src_ref=s0_ref.at[pl.ds(ts * 4 + tp, 1)], dst_ref=r0_ref.at[pl.ds(me, 1)],
            send_sem=s0sem, recv_sem=r0sem, device_id=(ts, tp), device_id_type=MESH,
        ).start()
    own0.start()

    def scatter(side, x):
        hi = x.astype(bf16)
        lo = (x - hi.astype(f32)).astype(bf16)
        total = jnp.zeros((128, 128), f32)
        for t in range(32):
            parts = []
            for i in (2 * t, 2 * t + 1):
                m = rmask_ref[side, i]
                parts.append(jnp.concatenate(
                    [m * jnp.broadcast_to(hi[i:i + 1], (64, 128)), m * jnp.broadcast_to(lo[i:i + 1], (64, 128))], axis=0))
            total = total + jnp.dot(
                jnp.concatenate(parts, axis=1), c_ref[side, t * 256:(t + 1) * 256, :], preferred_element_type=f32)
        return total[:64] + total[64:]

    def gather(side, v):
        hi = v.astype(bf16)
        lo = (v - hi.astype(f32)).astype(bf16)
        lhs = jnp.concatenate([hi, lo], axis=0)
        for t in range(32):
            p = jnp.dot(lhs, ct_ref[side, :, t * 256:(t + 1) * 256], preferred_element_type=f32)
            p = p[:64] + p[64:]
            for u in range(2):
                i = 2 * t + u
                read = jnp.sum(p[:, u * 128:(u + 1) * 128] * rmask_ref[side, i].astype(f32), axis=0, keepdims=True)
                s_ref[side, i:i + 1, :] = read * gain_ref[side, i:i + 1, :]

    def received(buffer):
        a, b = buffer[:64], buffer[64:]
        return jnp.where(lane64 < 64, pltpu.roll(a, 64 * half, 1), pltpu.roll(b, 64 * (1 - half), 1))

    def membrane(side, v):
        vh = 0.5 * v

        def pair(j, sums):
            conduct, driven = sums
            for u in range(2):
                k = 2 * j + u
                w = vh - prm_ref[0, k]
                factor = jnp.exp2(prm_ref[1, k] + prm_ref[2, k] * jnp.tanh(w))
                hc = prm_ref[3, k]
                swing = hc * jnp.tanh(w + w)
                steady = hc + swing if u == 0 else hc - swing
                old = y_ref[side, k].reshape(64, 128)
                new = steady + (old - steady) * factor
                y_ref[side, k] = new.reshape(4, 16, 128)
                conduct = conduct + new
                driven = driven + prm_ref[4, k] * new
            return conduct, driven

        zero = jnp.zeros((64, 128), f32)
        conduct, driven = lax.fori_loop(0, 20, pair, (zero, zero))
        return v * conduct - driven

    row16 = iota((16, 128), 0)
    lane16 = iota((16, 128), 1)

    def tissue_lap(par, slot):
        tiles = [v_ref[0, par, t] for t in range(4)]
        low = jnp.where(slab == 0, tiles[0], hb_ref[0, slot, 0])
        high = jnp.where(slab == 31, tiles[3], hb_ref[0, slot, 1])
        around = [low] + tiles + [high]
        out = []
        for t in range(4):
            here = tiles[t]
            ylo = jnp.where(plane == 0, here[0:1], hy_ref[slot, 0, t, 0:1, :])
            yhi = jnp.where(plane == 3, here[15:16], hy_ref[slot, 1, t, 0:1, :])
            total = around[t] + around[t + 2]
            total = total + jnp.where(row16 == 0, jnp.broadcast_to(ylo, (16, 128)), pltpu.roll(here, 1, 0))
            total = total + jnp.where(row16 == 15, jnp.broadcast_to(yhi, (16, 128)), pltpu.roll(here, 15, 0))
            total = total + jnp.where(lane16 == 0, here, pltpu.roll(here, 1, 1))
            total = total + jnp.where(lane16 == 127, here, pltpu.roll(here, 127, 1))
            out.append(total - 6.0 * here)
        return jnp.concatenate(out, axis=0)

    def fibre_lap(par, slot):
        tiles = [v_ref[1, par, t] for t in range(4)]
        around = [hb_ref[1, slot, 0]] + tiles + [hb_ref[1, slot, 1]]
        right = [pltpu.roll(a, 1, 1) for a in around[:5]]
        left = [pltpu.roll(a, 127, 1) for a in around[1:]]
        right[0] = jnp.where(plane == 0, tiles[0], right[0])
        left[4] = jnp.where(plane == 3, tiles[3], left[4])
        out = []
        for t in range(4):
            total = jnp.where(lane16 == 0, right[t], right[t + 1])
            total = total + jnp.where(lane16 == 127, left[t + 1], left[t])
            out.append(total - 2.0 * tiles[t])
        return jnp.concatenate(out, axis=0)

    def wait_rows(sem, rows):
        pltpu.make_async_copy(r0_ref.at[pl.ds(0, rows)], r0_ref.at[pl.ds(0, rows)], sem).wait()

    def wait_sends(side):
        wait_rows(ssem.at[side], 127)
        pltpu.make_async_copy(hb_ref.at[0, 0], hb_ref.at[0, 0], hssem.at[side]).wait()

        @pl.when(side == 0)
        def _():
            pltpu.make_async_copy(
                hy_ref.at[0, :, :, pl.ds(0, 1)], hy_ref.at[0, :, :, pl.ds(0, 1)], hssem.at[2]).wait()

    def act(m, carry):
        n = m // 2 - 1
        side = lax.rem(lax.rem(m, 2) + n + 2, 2)
        other = 1 - side
        par, slot = lax.rem(n + 2, 2), lax.rem(n + 4, 4)
        nxt, nslot = 1 - par, lax.rem(n + 5, 4)

        @pl.when(n >= 0)
        def _():
            v = v_ref[side, par].reshape(64, 128)
            ionic = membrane(side, v)
            pltpu.make_async_copy(hb_ref.at[0, 0], hb_ref.at[0, 0], hrsem.at[side, slot]).wait()

            def rest(lap):
                drift = d_ref[side].reshape(64, 128) * lap - ionic - gsum_ref[side] * v
                wait_rows(rsem.at[side, par], 127)
                x = received(r_ref[side, par]) * gain_ref[side]
                v_ref[side, nxt] = (v + DT * (drift + scatter(side, x))).reshape(4, 16, 128)

            @pl.when(side == 0)
            def _():
                pltpu.make_async_copy(
                    hy_ref.at[0, :, :, pl.ds(0, 1)], hy_ref.at[0, :, :, pl.ds(0, 1)], hrsem.at[2, slot]).wait()
                graw_ref[2] = tissue_lap(par, slot)

            @pl.when(side == 1)
            def _():
                graw_ref[2] = fibre_lap(par, slot)

            rest(graw_ref[2])

        @pl.when(n < 0)
        def _():
            @pl.when(side == 0)
            def _():
                wait_rows(r0sem, 128)
                table = r0_ref[...]
                cell = low_pair(table).astype(i32)
                row_ref[0] = cell // 128
                lane_ref[0] = lax.rem(cell, 128)
                graw_ref[0] = high_pair(table)

            def build(i, carry):
                at = pl.ds(i, 1)
                cols = pl.ds(pl.multiple_of(i * 128, 128), 128)
                rmask_ref[side, i] = jnp.where(
                    sub64 == jnp.broadcast_to(row_ref[side, at, :], (64, 128)), 1.0, 0.0).astype(bf16)
                ct_ref[side, :, cols] = jnp.where(
                    sub == jnp.broadcast_to(lane_ref[side, at, :], (128, 128)), 1.0, 0.0).astype(bf16)
                return carry

            lax.fori_loop(0, 64, build, 0)

        @pl.when(n < STEPS - 1)
        def _():
            @pl.when(n >= 0)
            def _():
                wait_sends(side)

            gather(side, v_ref[side, nxt].reshape(64, 128))
            r_ref[other, nxt, pl.ds(me, 1), :] = s_ref[side, pl.ds(q_me, 1), :]
            for ts, tp in peers:
                pltpu.make_async_remote_copy(
                    src_ref=s_ref.at[side, pl.ds(lax.rem(ts, 16) * 4 + tp, 1)],
                    dst_ref=r_ref.at[other, nxt, pl.ds(me, 1)],
                    send_sem=ssem.at[side], recv_sem=rsem.at[other, nxt],
                    device_id=(ts, tp), device_id_type=MESH,
                ).start()
            for up in (1, 0):
                ts = jnp.where(side == 0, lax.rem(slab + (1 if up else 31), 32), slab)
                tp = jnp.where(side == 0, plane, lax.rem(plane + (1 if up else 3), 4))
                pltpu.make_async_remote_copy(
                    src_ref=v_ref.at[side, nxt, 3 if up else 0], dst_ref=hb_ref.at[side, nslot, 1 - up],
                    send_sem=hssem.at[side], recv_sem=hrsem.at[side, nslot],
                    device_id=(ts, tp), device_id_type=MESH,
                ).start()

            @pl.when(side == 0)
            def _():
                for up in (1, 0):
                    pltpu.make_async_remote_copy(
                        src_ref=v_ref.at[0, nxt, :, pl.ds(15 if up else 0, 1)],
                        dst_ref=hy_ref.at[nslot, 1 - up, :, pl.ds(0, 1)],
                        send_sem=hssem.at[2], recv_sem=hrsem.at[2, nslot],
                        device_id=(slab, lax.rem(plane + (1 if up else 3), 4)), device_id_type=MESH,
                    ).start()

        @pl.when(n < 0)
        def _():
            def flip(i, carry):
                here = jnp.where(
                    sub == jnp.broadcast_to(lane_ref[side, pl.ds(i, 1), :], (128, 128)), 1.0, 0.0)
                c_ref[side, pl.ds(pl.multiple_of(i * 128, 128), 128), :] = here.T.astype(bf16)
                return carry

            lax.fori_loop(0, 64, flip, 0)
            gsum_ref[side] = scatter(side, graw_ref[side])

            @pl.when(side == 0)
            def _():
                loads[0].wait()

            @pl.when(side == 1)
            def _():
                for copy in loads[1:]:
                    copy.wait()

            def scale(k, carry):
                y_ref[side, k] = y_ref[side, k] * prm_ref[5, k]
                return carry

            lax.fori_loop(0, 40, scale, 0)

        return carry

    lax.fori_loop(0, 2 * STEPS + 2, act, 0)
    wait_rows(s0sem, 127)
    wait_sends(0)
    wait_sends(1)
    to_ref[...] = v_ref[0, STEPS % 2]
    for t in range(4):
        fo_ref[:, t * 128:(t + 1) * 128] = v_ref[1, STEPS % 2, t]


def body(
    tissue_v, tissue_gates, tissue_diff, fibre_v, fibre_gates, fibre_diff,
    gate_half, gate_rate, gate_cond, gate_rev, junc_cond,
    junc_fibre, junc_fcell, junc_owner, junc_tcell, junc_class,
):
    vmem, smem = pl.BlockSpec(memory_space=pltpu.VMEM), pl.BlockSpec(memory_space=pltpu.SMEM)
    anywhere = pl.BlockSpec(memory_space=pl.ANY)
    junctions = [a.reshape(32, 128) for a in (junc_fibre, junc_fcell, junc_owner[:, 0], junc_tcell, junc_class)]
    dma = pltpu.SemaphoreType.DMA
    return pl.pallas_call(
        kernel,
        out_shape=(jax.ShapeDtypeStruct((4, 16, 128), f32), jax.ShapeDtypeStruct((16, 512), f32)),
        in_specs=[vmem] * 4 + [anywhere] * 2 + [smem] * 5 + [vmem] * 5,
        out_specs=(vmem, vmem),
        scratch_shapes=[
            pltpu.VMEM((2, 2, 4, 16, 128), f32),
            pltpu.VMEM((2, 4, 16, 128), f32),
            pltpu.VMEM((2, 40, 4, 16, 128), f32),
            pltpu.SMEM((6, 40), f32),
            pltpu.VMEM((128, 4096), bf16),
            pltpu.VMEM((384, 4096), bf16),
            pltpu.VMEM((2, 64, 64, 128), bf16),
            pltpu.VMEM((2, 128, 8192), bf16),
            pltpu.VMEM((2, 8192, 128), bf16),
            pltpu.VMEM((2, 64, 128), i32),
            pltpu.VMEM((2, 64, 128), i32),
            pltpu.VMEM((2, 64, 128), f32),
            pltpu.VMEM((2, 64, 128), f32),
            pltpu.VMEM((3, 64, 128), f32),
            pltpu.VMEM((128, 128), f32),
            pltpu.VMEM((128, 128), f32),
            pltpu.VMEM((2, 64, 128), f32),
            pltpu.VMEM((2, 2, 128, 128), f32),
            pltpu.VMEM((2, 4, 2, 16, 128), f32),
            pltpu.VMEM((4, 2, 4, 8, 128), f32),
            dma((5,)), dma, dma, dma((2,)), dma((2, 2)), dma((3,)), dma((3, 4)),
        ],
        compiler_params=pltpu.CompilerParams(collective_id=0, has_side_effects=True),
    )(
        tissue_v, tissue_diff, fibre_v, fibre_diff, tissue_gates, fibre_gates,
        gate_half, gate_rate, gate_cond, gate_rev, junc_cond, *junctions,
    )


def solution(mesh):
    both = P(("slab", "plane"))
    in_specs = (
        P("slab", "plane", None), P(None, "slab", "plane", None), P("slab", "plane", None),
        P("slab", "plane"), P(None, "slab", "plane"), P("slab", "plane"),
        P(), P(), P(), P(), P(), both, both, P(("slab", "plane"), None), both, both,
    )
    out_specs = (P("slab", "plane", None), P("slab", "plane"))
    return jax.shard_map(body, mesh=mesh, in_specs=in_specs, out_specs=out_specs, check_vma=False)
```

time: 876 us -> 169 us (0.19)
  starting transfers between devices: 382 us -> 0 us
  matrix products: 354 us -> 0 us
  Pallas kernels: 0 us -> 166 us
  local copies, waits for them, and re-layouts: 65.3 us -> 2.75 us
  other arithmetic: 52.7 us -> 0 us
  waiting for transfers between devices: 9.96 us -> 0 us
    dot_general x140 -> x0, matrix products: 354 us -> none  [the longest x42 137 us: place_values(): lax.dot_general(row_onehot, weighted, (((0,), (0,)), ((), ())), precision...]
    ppermute x84 -> x0, starting transfers between devices: 212 us -> none  [the longest x28 92.8 us: extended(): lax.ppermute(last, axis, up)]
    all_to_all x15 -> x0, starting transfers between devices: 170 us -> none  [the longest x14 159 us: trade_both(): lax.all_to_all(paired, ('slab', 'plane'), split_axis=1, concat_axis=1, ti...]
    pallas_call x0 -> x1, Pallas kernels: none -> 166 us  [body(): pl.pallas_call(kernel, out_shape=(jax.ShapeDtypeStruct((4, 16, 128), f32)...]
    add x74 -> x0, other arithmetic: 37.6 us -> none  [the longest x28 34.6 us: membrane(): renewed = steady + (gates - steady) * decay_factor]
    scatter x2 -> x0, local copies, waits for them, and re-layouts: 31.4 us -> none  [the longest x1 15.9 us: body(): jnp.zeros((devices * capacity,), jnp.int32).at[slot_index].set(junc_tcell)]
    while x84 -> x0, local copies, waits for them, and re-layouts: 12.8 us -> none
    all_to_all x15 -> x0, other arithmetic: 12 us -> none  [the longest x14 11.2 us: trade_both(): lax.all_to_all(paired, ('slab', 'plane'), split_axis=1, concat_axis=1, ti...]
  transfers between devices with their start and end apart: 99 -> 0, of which waited for: 1 -> 0; matrix products, arithmetic and copies ran while one was open for 34% -> 0% of each run, Pallas kernels for 0% -> 0%
where the time goes in v1:
time: 169 us
  Pallas kernels  166 us (98%)
  local copies, waits for them, and re-layouts  2.75 us (2%)
    pallas_call x1, Pallas kernels, body(): pl.pallas_call(kernel, out_shape=(jax.ShapeDtypeStruct((4, 16, 128), f32)...  166 us

profile of v1, /device:TPU:1, one launch (start us, length us, event | category | flops | bytes accessed | tf_op | source)
XLA Modules:
  0.0 169.2 jit_solution(11075715013421739261)
XLA Ops:
  0.6 165.8 %shard_map.167 = (f32[4,16,128]{2,1,0:T(8,128)}, f32[16,512]{1,0:T(8,128)}) custom-call(f32[4,16,128]{2,1,0:T(8,128)} %tv_ref.1, f32[4,16,128]{2,1,0:T(8,128)} %td_ref.1, f32[16,512]{1,0:T(8,128)} %fv_ref.1, f32[16,512]{1,0:T(8,128)} %fd_ref.1, f32[40,4,16,128]{3,2,1,0:T(8,128)} %tg_ref.1, f32[40,16,512]{2,1,0:T(8,128)} %fg_ref.1, f32[40]{0:T(128)} %half_ref.1, ...), custom_call_target="tpu_custom_call" | custom-call | tf_op jit(solution)/shard_map/pallas_call | solution.py:378
  166.4 1.4 copy.20
  167.8 1.4 copy.21

commit v2 on v1

v2 whole, which is shorter than its diff:
```python
import jax
import jax.numpy as jnp
import numpy as np
from jax import lax
from jax.experimental import pallas as pl
from jax.experimental.pallas import tpu as pltpu
from jax.sharding import PartitionSpec as P

STEPS = 14
DT = 0.1
PARTS = 1
LOG2E = 1.4426950408889634
MESH = pl.DeviceIdType.MESH
f32, bf16, i32 = jnp.float32, jnp.bfloat16, jnp.int32


def rank_table():
    ring = lambda d: min(d, 4 - d)
    every = [(a, b, c, d) for a in range(4) for b in range(4) for c in range(2) for d in range(4)]
    far = lambda o: ring(o[0]) + ring(o[1]) + ring(o[3]) + 0.1 * o[2]
    streams, seen = ([], []), set()
    for o in sorted(every, key=lambda o: -far(o)):
        if o in seen:
            continue
        group = [o] if negative(o) == o else [o, negative(o)]
        seen.update(group)
        to = 0 if len(streams[0]) <= len(streams[1]) else 1
        if len(streams[to]) + len(group) > 64:
            to = 1 - to
        streams[to].extend(group)
    return streams[0] + streams[1]


def negative(o):
    return (-o[0] % 4, -o[1] % 4, o[2], -o[3] % 4)


RANKS = rank_table()
RANK_OF = {o: r for r, o in enumerate(RANKS)}
HERE = RANK_OF[(0, 0, 0, 0)]


def iota(shape, dim):
    return lax.broadcasted_iota(i32, shape, dim)


def kernel(
    tv_ref, td_ref, fv_ref, fd_ref, tg_ref, fg_ref,
    half_ref, rate_ref, cond_ref, rev_ref, jcond_ref,
    jf_ref, jc_ref, jo_ref, jt_ref, jk_ref, code_ref,
    to_ref, fo_ref,
    v_ref, d_ref, y_ref, prm_ref,
    oht_ref, kv_ref, rmask_ref, ct_ref, c_ref,
    row_ref, lane_ref, gain_ref, gsum_ref, graw_ref,
    s0_ref, r0_ref, s_ref, r_ref, hb_ref, hy_ref,
    gsem, s0sem, r0sem, ssem, rsem, hssem, hrsem,
):
    slab, plane = lax.axis_index("slab"), lax.axis_index("plane")
    z, y, core = slab // 8, lax.rem(slab // 2, 4), lax.rem(slab, 2)
    zs = [lax.rem(z + d, 4) * 8 for d in range(4)]
    ys = [lax.rem(y + d, 4) * 2 for d in range(4)]
    cs = [lax.rem(core + d, 2) for d in range(2)]
    xs = [lax.rem(plane + d, 4) for d in range(4)]

    def device(rank):
        a, b, c, d = RANKS[rank]
        return (zs[a] + ys[b] + cs[c], xs[d])

    peers = sorted((r for r in range(128) if r != HERE), key=lambda r: r % 64)

    loads = [pltpu.make_async_copy(tg_ref, y_ref.at[0], gsem.at[0])]
    for t in range(4):
        loads.append(pltpu.make_async_copy(fg_ref.at[:, :, pl.ds(t * 128, 128)], y_ref.at[1, :, t], gsem.at[1 + t]))
    for copy in loads:
        copy.start()

    barrier = pltpu.get_barrier_semaphore()

    for r in peers:
        pl.semaphore_signal(barrier, inc=1, device_id=device(r), device_id_type=MESH)

    def params(k, carry):
        rate, cond = rate_ref[k], cond_ref[k]
        prm_ref[6 * k + 0] = 0.5 * half_ref[k]
        prm_ref[6 * k + 1] = rate * (-1.5 * DT * LOG2E)
        prm_ref[6 * k + 2] = rate * (-0.5 * DT * LOG2E)
        prm_ref[6 * k + 3] = 0.5 * cond
        prm_ref[6 * k + 4] = rev_ref[k]
        prm_ref[6 * k + 5] = cond
        return carry

    lax.fori_loop(0, 40, params, 0)

    v_ref[0, 0] = tv_ref[...]
    d_ref[0] = td_ref[...]
    for t in range(4):
        v_ref[1, 0, t] = fv_ref[:, t * 128:(t + 1) * 128]
        d_ref[1, t] = fd_ref[:, t * 128:(t + 1) * 128]

    sub = iota((128, 128), 0)
    sub64 = iota((64, 128), 0)
    lane = iota((128, 128), 1)
    lane64 = iota((64, 128), 1)
    before = jnp.concatenate([jnp.where(sub < lane, 1.0, 0.0), jnp.ones((128, 128), f32)], axis=1).astype(bf16)

    def chunks(c4, count):
        for u in range(4):
            c = c4 * 4 + u
            at = pl.ds(c, 1)
            cols = pl.ds(pl.multiple_of(c * 128, 128), 128)
            owner = jo_ref[at, :]
            relative = (
                lax.rem(owner // 32 + 4 - z, 4) * 32 + lax.rem(lax.rem(owner // 8, 4) + 4 - y, 4) * 8
                + lax.rem(lax.rem(owner // 4, 2) + 2 - core, 2) * 4 + lax.rem(lax.rem(owner, 4) + 4 - plane, 4))
            hit = code_ref[...] == jnp.broadcast_to(relative, (128, 128))
            onehot = jnp.where(hit, 1.0, 0.0).astype(bf16)
            oht_ref[:, cols] = onehot
            seen = jnp.dot(onehot, before, preferred_element_type=f32)
            rank = jnp.sum(jnp.where(hit, seen[:, :128] + count, 0.0), axis=0, keepdims=True).astype(i32)
            place = sub64 == jnp.broadcast_to(rank, (64, 128))
            cell, fcell = jt_ref[at, :], jc_ref[at, :]
            planes = (
                cell // 128, jk_ref[at, :] + 1, lax.rem(cell, 128), jnp.zeros_like(cell),
                (fcell // 128) * 16 + jf_ref[at, :], lax.rem(fcell, 128))
            for p, value in enumerate(planes):
                value = jnp.broadcast_to(value.astype(f32), (64, 128))
                kv_ref[p * 64:(p + 1) * 64, cols] = jnp.where(place, value, 0.0).astype(bf16)
            count = count + seen[:, 128:]
        return count

    lax.fori_loop(0, 8, chunks, jnp.zeros((128, 128), f32))
    slots = lax.dot_general(oht_ref[...], kv_ref[...], (((1,), (1,)), ((), ())), preferred_element_type=f32)
    first, second, third = slots[:, :128], slots[:, 128:256], slots[:, 256:]
    gain = jnp.zeros((128, 128), f32)
    for k in range(8):
        gain = jnp.where(first == float(k + 1), jcond_ref[k], gain)
    s0_ref[...] = jnp.where(lane < 64, first * 128.0 + second, gain)

    def turn(array):
        return pltpu.roll(array, 64, 1)

    def low_pair(array):
        return jnp.where(lane64 < 64, array[:64], turn(array[64:]))

    def high_pair(array):
        return jnp.where(lane64 < 64, turn(array[:64]), array[64:])

    row_ref[1] = low_pair(third).astype(i32)
    lane_ref[1] = high_pair(third).astype(i32)
    gain_ref[1] = high_pair(s0_ref[...])
    gain_ref[0] = jnp.ones((64, 128), f32)
    graw_ref[1] = gain_ref[1]

    def send_tables():
        pl.semaphore_wait(barrier, 127)
        for r in peers:
            pltpu.make_async_remote_copy(
                src_ref=s0_ref.at[pl.ds(r, 1)], dst_ref=r0_ref.at[pl.ds(RANK_OF[negative(RANKS[r])], 1)],
                send_sem=s0sem, recv_sem=r0sem, device_id=device(r), device_id_type=MESH,
            ).start()
        r0_ref[HERE:HERE + 1, :] = s0_ref[HERE:HERE + 1, :]

    def send_row(side, nxt, i):
        for r in (i, i + 64):
            if r == HERE:
                r_ref[1 - side, nxt, HERE:HERE + 1, :] = s_ref[side, i:i + 1, :]
                continue
            to = RANK_OF[negative(RANKS[r])]
            pltpu.make_async_remote_copy(
                src_ref=s_ref.at[side, pl.ds(i, 1)], dst_ref=r_ref.at[1 - side, nxt, pl.ds(to, 1)],
                send_sem=ssem.at[side], recv_sem=rsem.at[1 - side, nxt, to % 64 // 32],
                device_id=device(r), device_id_type=MESH,
            ).start()

    def scatter(side, x, first):
        hi = x.astype(bf16)
        lo = (x - hi.astype(f32)).astype(bf16)
        total = jnp.zeros((128, 128), f32)
        for t in range(x.shape[0] // 2):
            parts = []
            for i in (2 * t, 2 * t + 1):
                m = rmask_ref[side, 2 * first + i]
                parts.append(jnp.concatenate(
                    [m * jnp.broadcast_to(hi[i:i + 1], (64, 128)), m * jnp.broadcast_to(lo[i:i + 1], (64, 128))], axis=0))
            at = (first + t) * 256
            total = total + jnp.dot(
                jnp.concatenate(parts, axis=1), c_ref[side, at:at + 256, :], preferred_element_type=f32)
        return total[:64] + total[64:]

    def gather(side, v, nxt, send):
        hi = v.astype(bf16)
        lo = (v - hi.astype(f32)).astype(bf16)
        lhs = jnp.concatenate([hi, lo], axis=0)
        for part in range(PARTS):
            rows = 64 // PARTS
            for t in range(part * rows // 2, (part + 1) * rows // 2):
                p = jnp.dot(lhs, ct_ref[side, :, t * 256:(t + 1) * 256], preferred_element_type=f32)
                p = p[:64] + p[64:]
                for u in range(2):
                    i = 2 * t + u
                    read = jnp.sum(p[:, u * 128:(u + 1) * 128] * rmask_ref[side, i].astype(f32), axis=0, keepdims=True)
                    s_ref[side, i:i + 1, :] = read * gain_ref[side, i:i + 1, :]
            for i in range(part * rows, (part + 1) * rows):
                send(side, nxt, i)

    def received(side, par, low):
        a = r_ref[side, par, low:low + 32, :]
        b = r_ref[side, par, 64 + low:96 + low, :]
        return jnp.where(lane64[:32] < 64, a, b) * gain_ref[side, low:low + 32, :]

    def membrane(side, par):
        out = []
        for h in range(2):
            v = v_ref[side, par, 2 * h:2 * h + 2].reshape(32, 128)
            vh = 0.5 * v

            def some(j, sums):
                conduct, driven = sums
                for u in range(8):
                    k = 8 * j + u
                    w = vh - prm_ref[6 * k]
                    factor = jnp.exp2(prm_ref[6 * k + 1] + prm_ref[6 * k + 2] * jnp.tanh(w))
                    hc = prm_ref[6 * k + 3]
                    swing = hc * jnp.tanh(w + w)
                    steady = hc + swing if u % 2 == 0 else hc - swing
                    old = y_ref[side, k, 2 * h:2 * h + 2].reshape(32, 128)
                    new = steady + (old - steady) * factor
                    y_ref[side, k, 2 * h:2 * h + 2] = new.reshape(2, 16, 128)
                    conduct = conduct + new
                    driven = driven + prm_ref[6 * k + 4] * new
                return conduct, driven

            zero = jnp.zeros((32, 128), f32)
            conduct, driven = lax.fori_loop(0, 5, some, (zero, zero))
            out.append(v * conduct - driven)
        return jnp.concatenate(out, axis=0)

    row16 = iota((16, 128), 0)
    lane16 = iota((16, 128), 1)

    def tissue_inner(par):
        tiles = [v_ref[0, par, t] for t in range(4)]
        around = [jnp.zeros((16, 128), f32)] + tiles + [jnp.zeros((16, 128), f32)]
        out = []
        for t in range(4):
            here = tiles[t]
            total = around[t] + around[t + 2]
            total = total + jnp.where(row16 == 0, 0.0, pltpu.roll(here, 1, 0))
            total = total + jnp.where(row16 == 15, 0.0, pltpu.roll(here, 15, 0))
            total = total + jnp.where(lane16 == 0, here, pltpu.roll(here, 1, 1))
            total = total + jnp.where(lane16 == 127, here, pltpu.roll(here, 127, 1))
            out.append(total - 6.0 * here)
        return jnp.concatenate(out, axis=0)

    def tissue_outer(par, slot):
        tiles = [v_ref[0, par, t] for t in range(4)]
        out = []
        for t in range(4):
            here = tiles[t]
            ylo = jnp.where(plane == 0, here[0:1], hy_ref[slot, 0, t, 0:1, :])
            yhi = jnp.where(plane == 3, here[15:16], hy_ref[slot, 1, t, 0:1, :])
            out.append(jnp.where(row16 == 0, jnp.broadcast_to(ylo, (16, 128)), 0.0)
                       + jnp.where(row16 == 15, jnp.broadcast_to(yhi, (16, 128)), 0.0))
        out[0] = out[0] + jnp.where(slab == 0, tiles[0], hb_ref[0, slot, 0])
        out[3] = out[3] + jnp.where(slab == 31, tiles[3], hb_ref[0, slot, 1])
        return jnp.concatenate(out, axis=0)

    def fibre_inner(par):
        tiles = [v_ref[1, par, t] for t in range(4)]
        right = [jnp.zeros((16, 128), f32)] + [pltpu.roll(a, 1, 1) for a in tiles]
        left = [pltpu.roll(a, 127, 1) for a in tiles] + [jnp.zeros((16, 128), f32)]
        out = []
        for t in range(4):
            total = jnp.where(lane16 == 0, right[t], right[t + 1])
            total = total + jnp.where(lane16 == 127, left[t + 1], left[t])
            out.append(total - 2.0 * tiles[t])
        return jnp.concatenate(out, axis=0)

    def fibre_outer(par, slot):
        right = jnp.where(plane == 0, v_ref[1, par, 0], pltpu.roll(hb_ref[1, slot, 0], 1, 1))
        left = jnp.where(plane == 3, v_ref[1, par, 3], pltpu.roll(hb_ref[1, slot, 1], 127, 1))
        none = jnp.zeros((16, 128), f32)
        return jnp.concatenate(
            [jnp.where(lane16 == 0, right, 0.0), none, none, jnp.where(lane16 == 127, left, 0.0)], axis=0)

    def wait_rows(sem, rows):
        pltpu.make_async_copy(r0_ref.at[pl.ds(0, rows)], r0_ref.at[pl.ds(0, rows)], sem).wait()

    def wait_tiles(sem):
        pltpu.make_async_copy(hb_ref.at[0, 0], hb_ref.at[0, 0], sem).wait()

    def wait_lines(sem):
        pltpu.make_async_copy(hy_ref.at[0, :, :, pl.ds(0, 1)], hy_ref.at[0, :, :, pl.ds(0, 1)], sem).wait()

    def wait_edges_sent(side):
        wait_tiles(hssem.at[side])

        @pl.when(side == 0)
        def _():
            wait_lines(hssem.at[2])

    def prepare(side):
        def flip(i8, carry):
            for u in range(8):
                i = i8 * 8 + u
                here = jnp.where(
                    sub == jnp.broadcast_to(lane_ref[side, pl.ds(i, 1), :], (128, 128)), 1.0, 0.0)
                c_ref[side, pl.ds(pl.multiple_of(i * 128, 128), 128), :] = here.T.astype(bf16)
            return carry

        lax.fori_loop(0, 8, flip, 0)
        gsum_ref[side] = scatter(side, graw_ref[side], 0)
        for copy in loads[:1] if side == 0 else loads[1:]:
            copy.wait()

        def scale(k, carry):
            y_ref[side, k] = y_ref[side, k] * prm_ref[6 * k + 5]
            return carry

        lax.fori_loop(0, 40, scale, 0)

    def act(m, carry):
        n = m // 2 - 1
        side = lax.rem(lax.rem(m, 2) + n + 2, 2)
        other = 1 - side
        par, slot = lax.rem(n + 2, 2), lax.rem(n + 4, 4)
        nxt, nslot = 1 - par, lax.rem(n + 5, 4)

        @pl.when(n >= 0)
        def _():
            v = v_ref[side, par].reshape(64, 128)
            graw_ref[2] = v - DT * (membrane(side, par) + gsum_ref[side] * v)
            diffusion = d_ref[side].reshape(64, 128)

            @pl.when(side == 0)
            def _():
                graw_ref[2] = graw_ref[2] + DT * diffusion * tissue_inner(par)

            @pl.when(side == 1)
            def _():
                graw_ref[2] = graw_ref[2] + DT * diffusion * fibre_inner(par)

            wait_rows(rsem.at[side, par, 1], 63)
            source = scatter(side, received(side, par, 32), 16)
            wait_rows(rsem.at[side, par, 0], 64)
            source = source + scatter(side, received(side, par, 0), 0)
            known = graw_ref[2] + DT * source
            wait_tiles(hrsem.at[side, slot])

            @pl.when(side == 0)
            def _():
                wait_lines(hrsem.at[2, slot])
                v_ref[0, nxt] = (known + DT * diffusion * tissue_outer(par, slot)).reshape(4, 16, 128)

            @pl.when(side == 1)
            def _():
                v_ref[1, nxt] = (known + DT * diffusion * fibre_outer(par, slot)).reshape(4, 16, 128)

        @pl.when(n < 0)
        def _():
            @pl.when(side == 0)
            def _():
                wait_rows(r0sem, 127)
                table = r0_ref[...]
                cell = low_pair(table).astype(i32)
                row_ref[0] = cell // 128
                lane_ref[0] = lax.rem(cell, 128)
                graw_ref[0] = high_pair(table)

            def build(i4, carry):
                for u in range(4):
                    i = i4 * 4 + u
                    at = pl.ds(i, 1)
                    cols = pl.ds(pl.multiple_of(i * 128, 128), 128)
                    rmask_ref[side, i] = jnp.where(
                        sub64 == jnp.broadcast_to(row_ref[side, at, :], (64, 128)), 1.0, 0.0).astype(bf16)
                    ct_ref[side, :, cols] = jnp.where(
                        sub == jnp.broadcast_to(lane_ref[side, at, :], (128, 128)), 1.0, 0.0).astype(bf16)
                return carry

            lax.fori_loop(0, 16, build, 0)

        @pl.when(m == 0)
        def _():
            prepare(1)
            send_tables()

        @pl.when(n < STEPS - 1)
        def _():
            @pl.when(n >= 0)
            def _():
                wait_edges_sent(side)
                wait_rows(ssem.at[side], 127)

            for up in (1, 0):
                ts = jnp.where(side == 0, lax.rem(slab + (1 if up else 31), 32), slab)
                tp = jnp.where(side == 0, plane, lax.rem(plane + (1 if up else 3), 4))
                pltpu.make_async_remote_copy(
                    src_ref=v_ref.at[side, nxt, 3 if up else 0], dst_ref=hb_ref.at[side, nslot, 1 - up],
                    send_sem=hssem.at[side], recv_sem=hrsem.at[side, nslot],
                    device_id=(ts, tp), device_id_type=MESH,
                ).start()

            @pl.when(side == 0)
            def _():
                for up in (1, 0):
                    pltpu.make_async_remote_copy(
                        src_ref=v_ref.at[0, nxt, :, pl.ds(15 if up else 0, 1)],
                        dst_ref=hy_ref.at[nslot, 1 - up, :, pl.ds(0, 1)],
                        send_sem=hssem.at[2], recv_sem=hrsem.at[2, nslot],
                        device_id=(slab, lax.rem(plane + (1 if up else 3), 4)), device_id_type=MESH,
                    ).start()

            gather(side, v_ref[side, nxt].reshape(64, 128), nxt, send_row)

        @pl.when(m == 1)
        def _():
            prepare(0)

        return carry

    lax.fori_loop(0, 2 * STEPS + 2, act, 0)
    wait_rows(s0sem, 127)
    for side in range(2):
        wait_rows(ssem.at[side], 127)
        wait_tiles(hssem.at[side])
    wait_lines(hssem.at[2])
    to_ref[...] = v_ref[0, STEPS % 2]
    for t in range(4):
        fo_ref[:, t * 128:(t + 1) * 128] = v_ref[1, STEPS % 2, t]


def body(
    tissue_v, tissue_gates, tissue_diff, fibre_v, fibre_gates, fibre_diff,
    gate_half, gate_rate, gate_cond, gate_rev, junc_cond,
    junc_fibre, junc_fcell, junc_owner, junc_tcell, junc_class,
):
    vmem, smem = pl.BlockSpec(memory_space=pltpu.VMEM), pl.BlockSpec(memory_space=pltpu.SMEM)
    anywhere = pl.BlockSpec(memory_space=pl.ANY)
    junctions = [a.reshape(32, 128) for a in (junc_fibre, junc_fcell, junc_owner[:, 0], junc_tcell, junc_class)]
    dma = pltpu.SemaphoreType.DMA
    codes = np.array([[a * 32 + b * 8 + c * 4 + d] * 128 for a, b, c, d in RANKS], np.int32)
    return pl.pallas_call(
        kernel,
        out_shape=(jax.ShapeDtypeStruct((4, 16, 128), f32), jax.ShapeDtypeStruct((16, 512), f32)),
        in_specs=[vmem] * 4 + [anywhere] * 2 + [smem] * 5 + [vmem] * 6,
        out_specs=(vmem, vmem),
        scratch_shapes=[
            pltpu.VMEM((2, 2, 4, 16, 128), f32),
            pltpu.VMEM((2, 4, 16, 128), f32),
            pltpu.VMEM((2, 40, 4, 16, 128), f32),
            pltpu.SMEM((240,), f32),
            pltpu.VMEM((128, 4096), bf16),
            pltpu.VMEM((384, 4096), bf16),
            pltpu.VMEM((2, 64, 64, 128), bf16),
            pltpu.VMEM((2, 128, 8192), bf16),
            pltpu.VMEM((2, 8192, 128), bf16),
            pltpu.VMEM((2, 64, 128), i32),
            pltpu.VMEM((2, 64, 128), i32),
            pltpu.VMEM((2, 64, 128), f32),
            pltpu.VMEM((2, 64, 128), f32),
            pltpu.VMEM((3, 64, 128), f32),
            pltpu.VMEM((128, 128), f32),
            pltpu.VMEM((128, 128), f32),
            pltpu.VMEM((2, 64, 128), f32),
            pltpu.VMEM((2, 2, 128, 128), f32),
            pltpu.VMEM((2, 4, 2, 16, 128), f32),
            pltpu.VMEM((4, 2, 4, 8, 128), f32),
            dma((5,)), dma, dma, dma((2,)), dma((2, 2, 2)), dma((3,)), dma((3, 4)),
        ],
        compiler_params=pltpu.CompilerParams(collective_id=0, has_side_effects=True),
    )(
        tissue_v, tissue_diff, fibre_v, fibre_diff, tissue_gates, fibre_gates,
        gate_half, gate_rate, gate_cond, gate_rev, junc_cond, *junctions, codes,
    )


def solution(mesh):
    both = P(("slab", "plane"))
    in_specs = (
        P("slab", "plane", None), P(None, "slab", "plane", None), P("slab", "plane", None),
        P("slab", "plane"), P(None, "slab", "plane"), P("slab", "plane"),
        P(), P(), P(), P(), P(), both, both, P(("slab", "plane"), None), both, both,
    )
    out_specs = (P("slab", "plane", None), P("slab", "plane"))
    return jax.shard_map(body, mesh=mesh, in_specs=in_specs, out_specs=out_specs, check_vma=False)
```

time: 169 us -> 132 us (0.78)
  Pallas kernels: 166 us -> 128 us
    pallas_call x1, Pallas kernels: 166 us -> 128 us  [body(): pl.pallas_call(kernel, out_shape=(jax.ShapeDtypeStruct((4, 16, 128), f32)...]
where the time goes in v2:
time: 132 us; the launch traced here: 131 us
  Pallas kernels  128 us (97%)
  local copies, waits for them, and re-layouts  2.75 us (2%)
    pallas_call x1, Pallas kernels, body(): pl.pallas_call(kernel, out_shape=(jax.ShapeDtypeStruct((4, 16, 128), f32)...  128 us
    unnamed x2, local copies, waits for them, and re-layouts  2.75 us

profile of v2, /device:TPU:1, one launch (start us, length us, event | category | flops | bytes accessed | tf_op | source)
XLA Modules:
  0.0 131.3 jit_solution(9768103228963353776)
XLA Ops:
  0.6 127.9 %shard_map.176 = (f32[4,16,128]{2,1,0:T(8,128)}, f32[16,512]{1,0:T(8,128)}) custom-call(f32[4,16,128]{2,1,0:T(8,128)} %tv_ref.1, f32[4,16,128]{2,1,0:T(8,128)} %td_ref.1, f32[16,512]{1,0:T(8,128)} %fv_ref.1, f32[16,512]{1,0:T(8,128)} %fd_ref.1, f32[40,4,16,128]{3,2,1,0:T(8,128)} %tg_ref.1, f32[40,16,512]{2,1,0:T(8,128)} %fg_ref.1, f32[40]{0:T(128)} %half_ref.1, ...), custom_call_target="tpu_custom_call" | custom-call | tf_op jit(solution)/shard_map/pallas_call | solution.py:443
  128.6 1.4 %copy.21 = f32[4,16,128]{2,1,0:T(8,128)} copy(f32[4,16,128]{2,1,0:T(8,128)} %get-tuple-element.4) | data formatting | bytes 65536
  129.9 1.4 %copy.22 = f32[16,512]{1,0:T(8,128)} copy(f32[16,512]{1,0:T(8,128)} %get-tuple-element.5) | data formatting | bytes 65536

commit v3 on v2

--- a/solution.py
+++ b/solution.py
@@ -8,7 +8,8 @@
 
 STEPS = 14
 DT = 0.1
-PARTS = 1
+CUTS = (0, 64)
+GROUPS = (0,)
 LOG2E = 1.4426950408889634
 MESH = pl.DeviceIdType.MESH
 f32, bf16, i32 = jnp.float32, jnp.bfloat16, jnp.int32
@@ -46,14 +47,16 @@
 
 def kernel(
     tv_ref, td_ref, fv_ref, fd_ref, tg_ref, fg_ref,
+    half_in, rate_in, cond_in, rev_in, jcond_in,
+    jf_in, jc_in, jo_in, jt_in, jk_in, code_in,
+    out_ref,
     half_ref, rate_ref, cond_ref, rev_ref, jcond_ref,
     jf_ref, jc_ref, jo_ref, jt_ref, jk_ref, code_ref,
-    to_ref, fo_ref,
     v_ref, d_ref, y_ref, prm_ref,
     oht_ref, kv_ref, rmask_ref, ct_ref, c_ref,
     row_ref, lane_ref, gain_ref, gsum_ref, graw_ref,
     s0_ref, r0_ref, s_ref, r_ref, hb_ref, hy_ref,
-    gsem, s0sem, r0sem, ssem, rsem, hssem, hrsem,
+    gsem, s0sem, r0sem, ssem, rsem, hssem, hrsem, isem,
 ):
     slab, plane = lax.axis_index("slab"), lax.axis_index("plane")
     z, y, core = slab // 8, lax.rem(slab // 2, 4), lax.rem(slab, 2)
@@ -68,16 +71,25 @@
 
     peers = sorted((r for r in range(128) if r != HERE), key=lambda r: r % 64)
 
+    barrier = pltpu.get_barrier_semaphore()
+    for r in peers:
+        pl.semaphore_signal(barrier, inc=1, device_id=device(r), device_id_type=MESH)
+
+    pairs = [
+        (jo_in, jo_ref), (code_in, code_ref), (jt_in, jt_ref), (jk_in, jk_ref), (jc_in, jc_ref), (jf_in, jf_ref),
+        (jcond_in, jcond_ref), (half_in, half_ref), (rate_in, rate_ref), (cond_in, cond_ref), (rev_in, rev_ref),
+        (tv_ref, v_ref.at[0, 0]), (td_ref, d_ref.at[0])]
+    for t in range(4):
+        pairs.append((fv_ref.at[:, pl.ds(t * 128, 128)], v_ref.at[1, 0, t]))
+        pairs.append((fd_ref.at[:, pl.ds(t * 128, 128)], d_ref.at[1, t]))
+    arrivals = [pltpu.make_async_copy(a, b, isem.at[k]) for k, (a, b) in enumerate(pairs)]
     loads = [pltpu.make_async_copy(tg_ref, y_ref.at[0], gsem.at[0])]
     for t in range(4):
         loads.append(pltpu.make_async_copy(fg_ref.at[:, :, pl.ds(t * 128, 128)], y_ref.at[1, :, t], gsem.at[1 + t]))
-    for copy in loads:
+    for copy in arrivals + loads:
         copy.start()
-
-    barrier = pltpu.get_barrier_semaphore()
-
-    for r in peers:
-        pl.semaphore_signal(barrier, inc=1, device_id=device(r), device_id_type=MESH)
+    for copy in arrivals:
+        copy.wait()
 
     def params(k, carry):
         rate, cond = rate_ref[k], cond_ref[k]
@@ -90,12 +102,6 @@
         return carry
 
     lax.fori_loop(0, 40, params, 0)
-
-    v_ref[0, 0] = tv_ref[...]
-    d_ref[0] = td_ref[...]
-    for t in range(4):
-        v_ref[1, 0, t] = fv_ref[:, t * 128:(t + 1) * 128]
-        d_ref[1, t] = fd_ref[:, t * 128:(t + 1) * 128]
 
     sub = iota((128, 128), 0)
     sub64 = iota((64, 128), 0)
@@ -168,45 +174,43 @@
             to = RANK_OF[negative(RANKS[r])]
             pltpu.make_async_remote_copy(
                 src_ref=s_ref.at[side, pl.ds(i, 1)], dst_ref=r_ref.at[1 - side, nxt, pl.ds(to, 1)],
-                send_sem=ssem.at[side], recv_sem=rsem.at[1 - side, nxt, to % 64 // 32],
+                send_sem=ssem.at[side], recv_sem=rsem.at[1 - side, nxt, sum(to % 64 < g for g in GROUPS)],
                 device_id=device(r), device_id_type=MESH,
             ).start()
 
-    def scatter(side, x, first):
+    def scatter(side, x, first, total):
         hi = x.astype(bf16)
         lo = (x - hi.astype(f32)).astype(bf16)
-        total = jnp.zeros((128, 128), f32)
-        for t in range(x.shape[0] // 2):
+        for t in range(0, x.shape[0], 2):
             parts = []
-            for i in (2 * t, 2 * t + 1):
-                m = rmask_ref[side, 2 * first + i]
+            for i in (t, t + 1):
+                m = rmask_ref[side, first + i]
                 parts.append(jnp.concatenate(
                     [m * jnp.broadcast_to(hi[i:i + 1], (64, 128)), m * jnp.broadcast_to(lo[i:i + 1], (64, 128))], axis=0))
-            at = (first + t) * 256
+            at = (first + t) * 128
             total = total + jnp.dot(
                 jnp.concatenate(parts, axis=1), c_ref[side, at:at + 256, :], preferred_element_type=f32)
-        return total[:64] + total[64:]
+        return total
 
     def gather(side, v, nxt, send):
         hi = v.astype(bf16)
         lo = (v - hi.astype(f32)).astype(bf16)
         lhs = jnp.concatenate([hi, lo], axis=0)
-        for part in range(PARTS):
-            rows = 64 // PARTS
-            for t in range(part * rows // 2, (part + 1) * rows // 2):
+        for start, stop in zip(CUTS, CUTS[1:]):
+            for t in range(start // 2, stop // 2):
                 p = jnp.dot(lhs, ct_ref[side, :, t * 256:(t + 1) * 256], preferred_element_type=f32)
                 p = p[:64] + p[64:]
                 for u in range(2):
                     i = 2 * t + u
                     read = jnp.sum(p[:, u * 128:(u + 1) * 128] * rmask_ref[side, i].astype(f32), axis=0, keepdims=True)
                     s_ref[side, i:i + 1, :] = read * gain_ref[side, i:i + 1, :]
-            for i in range(part * rows, (part + 1) * rows):
+            for i in range(start, stop):
                 send(side, nxt, i)
 
-    def received(side, par, low):
-        a = r_ref[side, par, low:low + 32, :]
-        b = r_ref[side, par, 64 + low:96 + low, :]
-        return jnp.where(lane64[:32] < 64, a, b) * gain_ref[side, low:low + 32, :]
+    def received(side, par, low, high):
+        a = r_ref[side, par, low:high, :]
+        b = r_ref[side, par, 64 + low:64 + high, :]
+        return jnp.where(lane64[:high - low] < 64, a, b) * gain_ref[side, low:high, :]
 
     def membrane(side, par):
         out = []
@@ -309,7 +313,8 @@
             return carry
 
         lax.fori_loop(0, 8, flip, 0)
-        gsum_ref[side] = scatter(side, graw_ref[side], 0)
+        total = scatter(side, graw_ref[side], 0, jnp.zeros((128, 128), f32))
+        gsum_ref[side] = total[:64] + total[64:]
         for copy in loads[:1] if side == 0 else loads[1:]:
             copy.wait()
 
@@ -340,11 +345,12 @@
             def _():
                 graw_ref[2] = graw_ref[2] + DT * diffusion * fibre_inner(par)
 
-            wait_rows(rsem.at[side, par, 1], 63)
-            source = scatter(side, received(side, par, 32), 16)
-            wait_rows(rsem.at[side, par, 0], 64)
-            source = source + scatter(side, received(side, par, 0), 0)
-            known = graw_ref[2] + DT * source
+            total, high = jnp.zeros((128, 128), f32), 64
+            for g, low in enumerate(GROUPS):
+                wait_rows(rsem.at[side, par, g], 2 * (high - low) - (low <= HERE % 64 < high))
+                total = scatter(side, received(side, par, low, high), low, total)
+                high = low
+            known = graw_ref[2] + DT * (total[:64] + total[64:])
             wait_tiles(hrsem.at[side, slot])
 
             @pl.when(side == 0)
@@ -425,9 +431,14 @@
         wait_rows(ssem.at[side], 127)
         wait_tiles(hssem.at[side])
     wait_lines(hssem.at[2])
-    to_ref[...] = v_ref[0, STEPS % 2]
+    out_ref[0] = v_ref[0, STEPS % 2]
+    out_ref[1] = v_ref[1, STEPS % 2]
+
+
+def unpack(in_ref, to_ref, fo_ref):
+    to_ref[...] = in_ref[0]
     for t in range(4):
-        fo_ref[:, t * 128:(t + 1) * 128] = v_ref[1, STEPS % 2, t]
+        fo_ref[:, t * 128:(t + 1) * 128] = in_ref[1, t]
 
 
 def body(
@@ -435,17 +446,18 @@
     gate_half, gate_rate, gate_cond, gate_rev, junc_cond,
     junc_fibre, junc_fcell, junc_owner, junc_tcell, junc_class,
 ):
-    vmem, smem = pl.BlockSpec(memory_space=pltpu.VMEM), pl.BlockSpec(memory_space=pltpu.SMEM)
+    vmem = pl.BlockSpec(memory_space=pltpu.VMEM)
     anywhere = pl.BlockSpec(memory_space=pl.ANY)
     junctions = [a.reshape(32, 128) for a in (junc_fibre, junc_fcell, junc_owner[:, 0], junc_tcell, junc_class)]
     dma = pltpu.SemaphoreType.DMA
     codes = np.array([[a * 32 + b * 8 + c * 4 + d] * 128 for a, b, c, d in RANKS], np.int32)
-    return pl.pallas_call(
+    held = pl.pallas_call(
         kernel,
-        out_shape=(jax.ShapeDtypeStruct((4, 16, 128), f32), jax.ShapeDtypeStruct((16, 512), f32)),
-        in_specs=[vmem] * 4 + [anywhere] * 2 + [smem] * 5 + [vmem] * 6,
-        out_specs=(vmem, vmem),
-        scratch_shapes=[
+        out_shape=jax.ShapeDtypeStruct((2, 4, 16, 128), f32),
+        in_specs=[anywhere] * 17,
+        out_specs=vmem,
+        scratch_shapes=[pltpu.SMEM((40,), f32)] * 4 + [pltpu.SMEM((8,), f32)] + [pltpu.VMEM((32, 128), i32)] * 5 + [
+            pltpu.VMEM((128, 128), i32),
             pltpu.VMEM((2, 2, 4, 16, 128), f32),
             pltpu.VMEM((2, 4, 16, 128), f32),
             pltpu.VMEM((2, 40, 4, 16, 128), f32),
@@ -466,13 +478,19 @@
             pltpu.VMEM((2, 2, 128, 128), f32),
             pltpu.VMEM((2, 4, 2, 16, 128), f32),
             pltpu.VMEM((4, 2, 4, 8, 128), f32),
-            dma((5,)), dma, dma, dma((2,)), dma((2, 2, 2)), dma((3,)), dma((3, 4)),
+            dma((5,)), dma, dma, dma((2,)), dma((2, 2, 3)), dma((3,)), dma((3, 4)), dma((21,)),
         ],
         compiler_params=pltpu.CompilerParams(collective_id=0, has_side_effects=True),
     )(
         tissue_v, tissue_diff, fibre_v, fibre_diff, tissue_gates, fibre_gates,
         gate_half, gate_rate, gate_cond, gate_rev, junc_cond, *junctions, codes,
     )
+    return pl.pallas_call(
+        unpack,
+        out_shape=(jax.ShapeDtypeStruct((4, 16, 128), f32), jax.ShapeDtypeStruct((16, 512), f32)),
+        in_specs=[vmem],
+        out_specs=(vmem, vmem),
+    )(held)
 
 
 def solution(mesh):

time: 132 us -> 128 us (0.970)
  local copies, waits for them, and re-layouts: 2.75 us -> 0 us
    unnamed x2 -> x0, local copies, waits for them, and re-layouts: 2.75 us -> none
    pallas_call x1 -> x2, Pallas kernels: 128 us -> 127 us  [the longest x1 126 us: body(): pl.pallas_call(kernel, out_shape=jax.ShapeDtypeStruct((2, 4, 16, 128), f3...]
where the time goes in v3:
time: 128 us
  Pallas kernels  127 us (99%)
    pallas_call x1, Pallas kernels, body(): pl.pallas_call(kernel, out_shape=jax.ShapeDtypeStruct((2, 4, 16, 128), f3...  126 us

profile of v3, /device:TPU:1, one launch (start us, length us, event | category | flops | bytes accessed | tf_op | source)
XLA Modules:
  0.0 128.1 jit_solution(13354445802289110216)
XLA Ops:
  0.6 126.0 %shard_map.176.in_ref = f32[2,4,16,128]{3,2,1,0:T(8,128)} custom-call(f32[4,16,128]{2,1,0:T(8,128)} %tv_ref.1, f32[4,16,128]{2,1,0:T(8,128)} %td_ref.1, f32[16,512]{1,0:T(8,128)} %fv_ref.1, f32[16,512]{1,0:T(8,128)} %fd_ref.1, f32[40,4,16,128]{3,2,1,0:T(8,128)} %tg_ref.1, f32[40,16,512]{2,1,0:T(8,128)} %fg_ref.1, f32[40]{0:T(128)} %half_in.1, f32[40]{0:T(128)} %rate_in.1, ...), custom_call_target="tpu_custom_call" | custom-call | tf_op jit(solution)/shard_map/pallas_call | solution.py:454
  126.6 1.5 %shard_map.177 = (f32[4,16,128]{2,1,0:T(8,128)}, f32[16,512]{1,0:T(8,128)}) custom-call(f32[2,4,16,128]{3,2,1,0:T(8,128)} %shard_map.176.in_ref), custom_call_target="tpu_custom_call" | custom-call | tf_op jit(solution)/shard_map/pallas_call | solution.py:488

commit v4 on v3

--- a/solution.py
+++ b/solution.py
@@ -388,7 +388,6 @@
 
         @pl.when(m == 0)
         def _():
-            prepare(1)
             send_tables()
 
         @pl.when(n < STEPS - 1)
@@ -418,6 +417,10 @@
                     ).start()
 
             gather(side, v_ref[side, nxt].reshape(64, 128), nxt, send_row)
+
+        @pl.when(m == 0)
+        def _():
+            prepare(1)
 
         @pl.when(m == 1)
         def _():

time: 128 us -> 126 us (0.984)
  Pallas kernels: 127 us -> 125 us
    pallas_call x1, Pallas kernels: 126 us -> 124 us  [body(): pl.pallas_call(kernel, out_shape=jax.ShapeDtypeStruct((2, 4, 16, 128), f3...]
where the time goes in v4:
time: 126 us
  Pallas kernels  125 us (99%)
    pallas_call x1, Pallas kernels, body(): pl.pallas_call(kernel, out_shape=jax.ShapeDtypeStruct((2, 4, 16, 128), f3...  124 us

profile of v4, /device:TPU:1, one launch (start us, length us, event | category | flops | bytes accessed | tf_op | source)
XLA Modules:
  0.0 126.0 jit_solution(10920788706693125688)
XLA Ops:
  0.6 123.8 %shard_map.176.in_ref = f32[2,4,16,128]{3,2,1,0:T(8,128)} custom-call(f32[4,16,128]{2,1,0:T(8,128)} %tv_ref.1, f32[4,16,128]{2,1,0:T(8,128)} %td_ref.1, f32[16,512]{1,0:T(8,128)} %fv_ref.1, f32[16,512]{1,0:T(8,128)} %fd_ref.1, f32[40,4,16,128]{3,2,1,0:T(8,128)} %tg_ref.1, f32[40,16,512]{2,1,0:T(8,128)} %fg_ref.1, f32[40]{0:T(128)} %half_in.1, f32[40]{0:T(128)} %rate_in.1, ...), custom_call_target="tpu_custom_call" | custom-call | tf_op jit(solution)/shard_map/pallas_call | solution.py:457
  124.5 1.5 %shard_map.177 = (f32[4,16,128]{2,1,0:T(8,128)}, f32[16,512]{1,0:T(8,128)}) custom-call(f32[2,4,16,128]{3,2,1,0:T(8,128)} %shard_map.176.in_ref), custom_call_target="tpu_custom_call" | custom-call | tf_op jit(solution)/shard_map/pallas_call | solution.py:491
